TPU v7x, 32 devices: a 4x4x1 block of a 4x4x8 slice. The times are simulated.
32 devices in a mesh: dp: 1 (over z), x: 4 (over y), y: 8 (over x, core).
Axes of the slice: x: 4, y: 4, z: 1, core: 2. Of those that a mesh axis runs over, the one named last changes fastest.
The devices are a block of a 4x4x8 slice.
Arguments:
- hidden: bfloat16 [1024, 1024], P('dp', 'x')
- w_qkv: bfloat16 [1024, 3072], P('x', 'y')
- b_qkv: bfloat16 [3072], P('y')
- w_out: bfloat16 [1024, 1024], P('y', 'x')
- b_out: bfloat16 [1024], P('x')
- attn_gain: bfloat16 [1024], P('x')
- attn_shift: bfloat16 [1024], P('x')
- w_up: bfloat16 [1024, 2, 4096], P('x', None, 'y')
- b_up: bfloat16 [2, 4096], P(None, 'y')
- w_down: bfloat16 [4096, 1024], P('y', 'x')
- b_down: bfloat16 [1024], P('x')
- mlp_gain: bfloat16 [1024], P('x')
- mlp_shift: bfloat16 [1024], P('x')
- k_cache: bfloat16 [1024, 64, 16, 64], P('dp', None, 'y')
- v_cache: bfloat16 [1024, 64, 16, 64], P('dp', None, 'y')
- positions: int32 [1024], P('dp')
- lengths: int32 [1024], P('dp')
Outputs:
- output 1: bfloat16 [1024, 1024], P('dp', 'x')
- output 2: bfloat16 [1024, 64, 16, 64], P('dp', None, 'y')
- output 3: bfloat16 [1024, 64, 16, 64], P('dp', None, 'y')
All inputs are finite; a program needn't handle non-finite values.
Results may differ from a plain program's by a relative error of at most 0.02.
Values are sent between devices in bfloat16 or wider.
A program may use at most 768 MiB of HBM per device.

v0:
```python
import math
import jax
import jax.numpy as jnp
from jax import lax
from jax.sharding import PartitionSpec as P

DEEP_ALPHA = math.sqrt(140.0)
LN_EPS = 1e-5
ROPE_BASE = 10000.0


def apply_rotary(head_vec, positions):
    head_dim = head_vec.shape[-1]
    half_dim = head_dim // 2
    inv_freq = ROPE_BASE ** (-2.0 * jnp.arange(half_dim, dtype=jnp.float32) / head_dim)
    angles = positions.astype(jnp.float32)[:, None] * inv_freq[None, :]
    cos_table = jnp.cos(angles)[:, None, :]
    sin_table = jnp.sin(angles)[:, None, :]
    vec_wide = head_vec.astype(jnp.float32)
    lower_half = vec_wide[..., :half_dim]
    upper_half = vec_wide[..., half_dim:]
    return jnp.concatenate([lower_half * cos_table - upper_half * sin_table, upper_half * cos_table + lower_half * sin_table], axis=-1).astype(jnp.bfloat16)


def write_slot(cache, new_rows, lengths):
    slot_hit = jnp.arange(cache.shape[1])[None, :, None, None] == lengths[:, None, None, None]
    return jnp.where(slot_hit, new_rows[:, None], cache)


def attend(query_rot, k_full, v_full, lengths):
    head_dim = query_rot.shape[-1]
    scores = jnp.einsum('bhd,bshd->bhs', query_rot, k_full, preferred_element_type=jnp.float32) * (head_dim ** -0.5)
    slot_ok = jnp.arange(k_full.shape[1])[None, None, :] <= lengths[:, None, None]
    scores = jnp.where(slot_ok, scores, -1e30)
    attn_probs = jax.nn.softmax(scores, axis=-1).astype(jnp.bfloat16)
    attn_mixed = jnp.einsum('bhs,bshd->bhd', attn_probs, v_full, preferred_element_type=jnp.float32)
    return attn_mixed.astype(jnp.bfloat16).reshape(query_rot.shape[0], -1)


def sharded_norm(h_val, gain, shift, width_all):
    moments = jnp.stack([jnp.sum(h_val, axis=1), jnp.sum(h_val * h_val, axis=1)], axis=1)
    moments = lax.psum(moments, 'x')
    mean_row = moments[:, 0:1] / width_all
    var_row = moments[:, 1:2] / width_all - mean_row * mean_row
    scaled = (h_val - mean_row) * lax.rsqrt(var_row + LN_EPS)
    return (scaled * gain.astype(jnp.float32) + shift.astype(jnp.float32)).astype(jnp.bfloat16)


def solution(mesh):
    x_size = mesh.shape['x']
    cache_spec = P('dp', None, 'y', None)
    width_spec = P('x')
    in_specs = (P('dp', 'x'), P('x', 'y'), P('y'), P('y', 'x'), width_spec, width_spec, width_spec, P('x', None, 'y'), P(None, 'y'), P('y', 'x'), width_spec, width_spec, width_spec, cache_spec, cache_spec, P('dp'), P('dp'))
    out_specs = (P('dp', 'x'), cache_spec, cache_spec)

    def local_step(hidden, w_qkv, b_qkv, w_out, b_out, attn_gain, attn_shift, w_up, b_up, w_down, b_down, mlp_gain, mlp_shift, k_cache, v_cache, positions, lengths):
        row_count, width_local = hidden.shape
        width_all = width_local * x_size
        local_heads, head_dim = k_cache.shape[2], k_cache.shape[3]
        qkv_part = jnp.dot(hidden, w_qkv, preferred_element_type=jnp.float32).astype(jnp.bfloat16)
        qkv_sum = lax.psum(qkv_part, 'x')
        qkv_vals = (qkv_sum.astype(jnp.float32) + b_qkv.astype(jnp.float32)).astype(jnp.bfloat16)
        qkv_vals = qkv_vals.reshape(row_count, local_heads, 3, head_dim)
        query_rot = apply_rotary(qkv_vals[:, :, 0], positions)
        k_full = write_slot(k_cache, apply_rotary(qkv_vals[:, :, 1], positions), lengths)
        v_full = write_slot(v_cache, qkv_vals[:, :, 2], lengths)
        attn_out = attend(query_rot, k_full, v_full, lengths)
        proj_part = jnp.dot(attn_out, w_out, preferred_element_type=jnp.float32).astype(jnp.bfloat16)
        proj_sum = lax.psum(proj_part, 'y')
        h_attn = DEEP_ALPHA * hidden.astype(jnp.float32) + proj_sum.astype(jnp.float32) + b_out.astype(jnp.float32)
        normed = sharded_norm(h_attn, attn_gain, attn_shift, width_all)
        up_part = jnp.einsum('bd,dtf->btf', normed, w_up, preferred_element_type=jnp.float32).astype(jnp.bfloat16)
        up_sum = lax.psum(up_part, 'x').astype(jnp.float32) + b_up.astype(jnp.float32)
        gated_act = (jax.nn.gelu(up_sum[:, 0], approximate=True) * up_sum[:, 1]).astype(jnp.bfloat16)
        down_part = jnp.dot(gated_act, w_down, preferred_element_type=jnp.float32).astype(jnp.bfloat16)
        down_sum = lax.psum(down_part, 'y')
        h_mlp = DEEP_ALPHA * normed.astype(jnp.float32) + down_sum.astype(jnp.float32) + b_down.astype(jnp.float32)
        result = sharded_norm(h_mlp, mlp_gain, mlp_shift, width_all)
        return result, k_full, v_full

    return jax.shard_map(local_step, mesh=mesh, in_specs=in_specs, out_specs=out_specs, check_vma=False)
```

profile of v0, /device:TPU:97, one launch (start us, length us, event | category | flops | bytes accessed | tf_op | source)
XLA Modules:
  0.0 291.8 jit_solution(10920133769603065484)
XLA Ops:
  7.2 0.0 copy-start
  7.2 0.1 all-reduce.5.cloned.1.call-start
  7.3 2.4 convolution_convert_fusion.1
  9.7 0.1 all-reduce.5.cloned.1.call-update
  9.8 0.1 all-reduce.7.cloned.1.call-start
  9.8 0.7 convert_element_type.97
  10.5 0.7 convert_element_type.101
  11.2 0.8 iota_compare_fusion.1
  12.0 0.5 multiply_cosine_fusion
  12.5 39.7 %all-reduce.5.cloned.1.call-done = bf16[1024,384]{1,0:T(8,128)(2,1)} async-done(((bf16[1024,384]{1,0:T(8,128)(2,1)}), bf16[1024,384]{1,0:T(8,128)(2,1)}) %all-reduce.5.cloned.1.call-update) | async-done | bytes 786448 | tf_op jit(solution)/shard_map/psum | solution.py:61
  52.3 1.3 add_convert_fusion
  53.6 0.3 copy.29
  53.9 0.1 slice_bitcast_fusion.2
  54.0 0.1 subtract_convert_fusion
  54.1 0.1 maximum_convert_fusion
  54.2 16.9 %multiply_reduce_fusion.1 = (f32[1024,2,64]{0,1,2:T(2,128)S(1)}, bf16[1024,64,2,64]{0,3,2,1:T(8,128)(2,1)}) fusion(f32[1024,2,64]{0,2,1:T(8,128)S(1)} %get-tuple-element.28, bf16[1024,64,2,64]{0,3,2,1:T(8,128)(2,1)} %param.30, bf16[1024,2,64]{0,2,1:T(8,128)(2,1)S(1)} %get-tuple-element.29, pred[1024,64]{0,1:T(8,128)(4,1)S(1)} %get-tuple-element.27), kind=kLoop, calls=%fused_computation.3 | loop fusion | flops 33423360 | bytes 34930688
  71.1 0.3 fusion.15
  71.5 0.4 copy.47
  71.9 0.0 copy-start.2
  71.9 0.0 copy-start.5
  71.9 0.0 copy-start.6
  71.9 0.0 copy-start.7
  71.9 0.0 copy-start.1
  71.9 17.7 %multiply_reduce_fusion = (bf16[1024,2,64]{0,2,1:T(8,128)(2,1)S(1)}, bf16[1024,64,2,64]{0,3,2,1:T(8,128)(2,1)}) fusion(f32[1024,2,64]{0,1,2:T(2,128)S(1)} %copy.47, bf16[1024,64,2,64]{0,3,2,1:T(8,128)(2,1)} %param.31, bf16[1024,2,64]{0,2,1:T(8,128)(2,1)S(1)} %get-tuple-element.11, pred[1024,64]{0,1:T(8,128)(4,1)S(1)} %get-tuple-element.27), kind=kLoop, calls=%fused_computation.2 | loop fusion | flops 33423360 | bytes 34668544 | tf_op jit(solution)/shard_map/bhs,bshd->bhd/dot_general | solution.py:36
  89.7 0.0 copy-done.2
  89.7 1.1 convolution_convert_fusion.3
  90.8 0.1 all-reduce.7.cloned.1.call-update
  90.9 0.1 all-reduce.9.cloned.1.call-start
  91.0 56.3 %all-reduce.7.cloned.1.call-done = bf16[1024,256]{1,0:T(8,128)(2,1)} async-done(((bf16[1024,256]{1,0:T(8,128)(2,1)}), bf16[1024,256]{1,0:T(8,128)(2,1)}) %all-reduce.7.cloned.1.call-update) | async-done | bytes 524304 | tf_op jit(solution)/shard_map/psum | solution.py:69
  147.3 1.5 fusion.17
  148.8 8.6 %psum.44 = f32[1024,2]{0,1:T(2,128)S(1)} all-reduce(f32[1024,2]{0,1:T(2,128)S(1)} %pad_maximum_fusion.1), channel_id=1, replica_groups=mesh['dp'=1,'x'=4,'y'=8] {'x'}, use_global_device_ids=true, to_apply=%region_6.7 | all-reduce | flops 2048 | bytes 16384 | tf_op jit(solution)/shard_map/psum | solution.py:42
  157.5 1.4 add_convert_fusion.2
  158.9 0.0 copy-done
  158.9 2.0 convolution_convert_fusion
  160.9 0.1 all-reduce.9.cloned.1.call-update
  161.0 0.1 all-reduce.11.cloned.1.call-start
  161.1 54.1 %all-reduce.9.cloned.1.call-done = bf16[1024,2,512]{2,0,1:T(8,128)(2,1)} async-done(((bf16[1024,2,512]{2,0,1:T(8,128)(2,1)}), bf16[1024,2,512]{2,0,1:T(8,128)(2,1)}) %all-reduce.9.cloned.1.call-update) | async-done | bytes 2097168 | tf_op jit(solution)/shard_map/psum | solution.py:73
  215.2 2.2 convert_add_fusion
  217.4 0.0 copy-start.8
  217.4 0.0 copy-start.9
  217.4 0.0 copy-start.10
  217.4 1.7 convolution_convert_fusion.2
  219.1 0.1 all-reduce.11.cloned.1.call-update
  219.2 0.0 copy-done.8
  219.2 53.7 %all-reduce.11.cloned.1.call-done = bf16[1024,256]{1,0:T(8,128)(2,1)} async-done(((bf16[1024,256]{1,0:T(8,128)(2,1)}), bf16[1024,256]{1,0:T(8,128)(2,1)}) %all-reduce.11.cloned.1.call-update) | async-done | bytes 524304 | tf_op jit(solution)/shard_map/psum | solution.py:76
  272.9 1.5 fusion.18
  274.4 8.6 %psum.47 = f32[1024,2]{0,1:T(2,128)S(1)} all-reduce(f32[1024,2]{0,1:T(2,128)S(1)} %pad_maximum_fusion.2), channel_id=1, replica_groups=mesh['dp'=1,'x'=4,'y'=8] {'x'}, use_global_device_ids=true, to_apply=%region_11.12 | all-reduce | flops 2048 | bytes 16384 | tf_op jit(solution)/shard_map/psum | solution.py:42
  283.1 2.2 add_convert_fusion.1
  (22 shorter events, 0.1 us)
Async XLA Ops:
  7.2 151.7 %copy-start = (bf16[256,2,512]{2,1,0:T(2,128)(2,1)S(1)}, bf16[256,2,512]{2,1,0:T(2,128)(2,1)}, u32[]{:S(2)}) copy-start(bf16[256,2,512]{2,1,0:T(2,128)(2,1)} %param.24) | copy-start | bytes 1572868
  7.2 45.1 %all-reduce.5.cloned.1.call-start = ((), (), s32[]{:S(2)}) async-start(), calls=%async_computation | async-start | bytes 1572864 | tf_op jit(solution)/shard_map/psum | solution.py:61
  9.8 137.6 %all-reduce.7.cloned.1.call-start = ((), (), s32[]{:S(2)}) async-start(), calls=%async_computation.1 | async-start | bytes 1048576 | tf_op jit(solution)/shard_map/psum | solution.py:69
  71.9 17.8 %copy-start.2 = (bf16[128,256]{1,0:T(8,128)(2,1)S(1)}, bf16[128,256]{1,0:T(8,128)(2,1)}, u32[]{:S(2)}) copy-start(bf16[128,256]{1,0:T(8,128)(2,1)} %param.20) | copy-start | bytes 196612
  71.9 19.0 %copy-start.5 = (bf16[256]{0:T(256)(128)(2,1)S(1)}, bf16[256]{0:T(256)(128)(2,1)}, u32[]{:S(2)}) copy-start(bf16[256]{0:T(256)(128)(2,1)} %param.21) | copy-start | bytes 1540
  71.9 19.0 %copy-start.6 = (bf16[256]{0:T(256)(128)(2,1)S(1)}, bf16[256]{0:T(256)(128)(2,1)}, u32[]{:S(2)}) copy-start(bf16[256]{0:T(256)(128)(2,1)} %param.22) | copy-start | bytes 1540
  71.9 19.1 %copy-start.7 = (bf16[256]{0:T(256)(128)(2,1)S(1)}, bf16[256]{0:T(256)(128)(2,1)}, u32[]{:S(2)}) copy-start(bf16[256]{0:T(256)(128)(2,1)} %param.23) | copy-start | bytes 1540
  71.9 75.4 %copy-start.1 = (bf16[1024,256]{1,0:T(8,128)(2,1)S(1)}, bf16[1024,256]{1,0:T(8,128)(2,1)}, u32[]{:S(2)}) copy-start(bf16[1024,256]{1,0:T(8,128)(2,1)} %param.17) | copy-start | bytes 1572868
  90.8 70.2 %copy-start.3 = (bf16[2,512]{1,0:T(2,128)(2,1)S(1)}, bf16[2,512]{1,0:T(2,128)(2,1)}, u32[]{:S(2)}) copy-start(bf16[2,512]{1,0:T(2,128)(2,1)} %param.25) | copy-start | bytes 6148
  90.9 124.3 %all-reduce.9.cloned.1.call-start = ((), (), s32[]{:S(2)}) async-start(), calls=%async_computation.2 | async-start | bytes 4194304 | tf_op jit(solution)/shard_map/psum | solution.py:73
  160.9 56.5 %copy-start.4 = (bf16[512,256]{1,0:T(8,128)(2,1)S(1)}, bf16[512,256]{1,0:T(8,128)(2,1)}, u32[]{:S(2)}) copy-start(bf16[512,256]{1,0:T(8,128)(2,1)} %param.26) | copy-start | bytes 786436
  161.0 112.0 %all-reduce.11.cloned.1.call-start = ((), (), s32[]{:S(2)}) async-start(), calls=%async_computation.3 | async-start | bytes 1048576 | tf_op jit(solution)/shard_map/psum | solution.py:76
  217.4 1.8 copy-start.8
  217.4 1.8 copy-start.9
  217.4 1.8 copy-start.10
Sparse Core Ops, SparseCore 0:
  11.0 41.2 all-reduce.4
  91.0 56.3 all-reduce.6
  161.1 54.0 all-reduce.8
  219.3 53.5 all-reduce.10
where the time goes:
time: 295 us; the launch traced here: 292 us
  waiting for transfers between devices  204 us (69%)
  other arithmetic  48 us (16%)
  blocking collectives  17.3 us (6%)
  between operations  14.1 us (5%)
  matrix products  7.27 us (2%)
    psum x1, waiting for transfers between devices, local_step(): proj_sum = lax.psum(proj_part, 'y')  56.3 us
    psum x1, waiting for transfers between devices, local_step(): lax.psum(up_part, 'x').astype(jnp.float32) + b_up.astype(jnp.float32)  54.1 us
    psum x1, waiting for transfers between devices, local_step(): down_sum = lax.psum(down_part, 'y')  53.7 us
    psum x1, waiting for transfers between devices, local_step(): qkv_sum = lax.psum(qkv_part, 'x')  39.7 us
    dot_general x1, other arithmetic, attend(): jnp.einsum('bhs,bshd->bhd', attn_probs, v_full, preferred_element_type=jn...  17.7 us
    psum x2, blocking collectives, sharded_norm(): moments = lax.psum(moments, 'x')  17.3 us
    unnamed x2, other arithmetic  17 us
  transfers between devices with their start and end apart: 4, of which 4 were waited for; matrix products, arithmetic and copies ran while one was open for 1% of the time, Pallas kernels for 0%

commit v1 on v0

v1 whole, which is shorter than its diff:
```python
import functools
import math
import jax
import jax.numpy as jnp
from jax import lax
from jax.experimental import pallas as pl
from jax.experimental.pallas import tpu as pltpu
from jax.sharding import PartitionSpec as P

DEEP_ALPHA = math.sqrt(140.0)
LN_EPS = 1e-5
ROPE_BASE = 10000.0
MESH = pl.DeviceIdType.MESH
CORES = 2
F32 = jnp.float32
BF16 = jnp.bfloat16


def layer_norm(h_val, gain, shift):
    mean_row = jnp.mean(h_val, axis=-1, keepdims=True)
    cent = h_val - mean_row
    var_row = jnp.mean(cent * cent, axis=-1, keepdims=True)
    return (cent * lax.rsqrt(var_row + LN_EPS) * gain + shift).astype(BF16)


def tail_kernel(nx, ny, attn_ref, hid_ref, wo_ref, vec_ref, wup_ref, bup_ref, wdn_ref, out_ref,
                part1, dbuf1, sbuf1, rbuf1, part2, dbuf2, sbuf2, rbuf2, zall, obuf, send, recv):
    nc = ny // CORES
    x, y = lax.axis_index('x'), lax.axis_index('y')
    core, chip = lax.rem(y, CORES), lax.div(y, CORES)
    partner = {'y': chip * CORES + (1 - core)}
    blk = core * nc + chip
    rows = hid_ref.shape[0]
    width = vec_ref.shape[2]

    def chip_at(d):
        return lax.rem(chip + d + nc, nc)

    def x_at(d):
        return lax.rem(x + d + nx, nx)

    def chip_dev(d):
        return {'y': chip_at(d) * CORES + core}

    def copy(src, dst, i, dev):
        return pltpu.make_async_remote_copy(src_ref=src, dst_ref=dst, send_sem=send.at[i], recv_sem=recv.at[i],
                                            device_id=dev, device_id_type=MESH)

    barrier = pltpu.get_barrier_semaphore()
    pl.semaphore_signal(barrier, inc=1, device_id=partner, device_id_type=MESH)
    for d in range(1, nc):
        pl.semaphore_signal(barrier, inc=1, device_id=chip_dev(d), device_id_type=MESH)
    for d in range(1, nx):
        pl.semaphore_signal(barrier, inc=1, device_id={'x': x_at(d)}, device_id_type=MESH)
    pl.semaphore_wait(barrier, nc + nx - 1)

    def vec(i):
        return jnp.concatenate([vec_ref[b, i:i + 1, :] for b in range(nx)], axis=1).astype(F32)

    def scatter_sum(part, dbuf, sbuf, rbuf, base):
        cp = copy(part.at[1 - core], dbuf, base, partner)
        cp.start()
        cp.wait()
        sbuf[...] = (part[core].astype(F32) + dbuf[...].astype(F32)).astype(BF16)
        cps = [copy(sbuf.at[chip_at(d)], rbuf.at[d - 1], base + d, chip_dev(d)) for d in range(1, nc)]
        for cp in cps:
            cp.start()
        total = sbuf[chip].astype(F32)
        for d in range(1, nc):
            cps[d - 1].wait()
            total = total + rbuf[d - 1].astype(F32)
        return total

    def share(buf_at, base):
        far = [copy(buf_at(blk), buf_at(blk), base + d - 1, chip_dev(d)) for d in range(1, nc)]
        for cp in far:
            cp.start()
        near = [copy(buf_at(blk), buf_at(blk), base + nc - 1, partner)]
        near[0].start()
        for d in range(1, nc):
            b = core * nc + chip_at(-d)
            copy(buf_at(b), buf_at(b), base + d - 1, chip_dev(d)).wait_recv()
            cp = copy(buf_at(b), buf_at(b), base + nc - 1 + d, partner)
            cp.start()
            near.append(cp)
        for d in range(nc):
            b = (1 - core) * nc + chip_at(-d)
            copy(buf_at(b), buf_at(b), base + nc - 1 + d, partner).wait_recv()
        for cp in far + near:
            cp.wait_send()

    per = 2 * nc - 1
    base1, base2, base3, base4, base5 = 0, nc, nc + per, 2 * nc + per, 2 * nc + per + nx

    for b in range(nx):
        res = jnp.dot(attn_ref[...], wo_ref[b], preferred_element_type=F32).astype(BF16)
        part1[:, :, :, b * width:(b + 1) * width] = res.reshape(CORES, nc, rows, width)
    total = scatter_sum(part1, dbuf1, sbuf1, rbuf1, base1)
    h_attn = DEEP_ALPHA * hid_ref[...].astype(F32) + total + vec(0)
    z_own = layer_norm(h_attn, vec(1), vec(2))
    zall[blk] = z_own
    share(lambda b: zall.at[b], base2)

    z = zall[...].reshape(ny * rows, nx * width)
    gate = bup_ref[0:1, :].astype(F32)
    val = bup_ref[1:2, :].astype(F32)
    for b in range(nx):
        zb = z[:, b * width:(b + 1) * width]
        gate = gate + jnp.dot(zb, wup_ref[b, 0], preferred_element_type=F32)
        val = val + jnp.dot(zb, wup_ref[b, 1], preferred_element_type=F32)
    g = (jax.nn.gelu(gate, approximate=True) * val).astype(BF16)
    for b in range(nx):
        res = jnp.dot(g, wdn_ref[b], preferred_element_type=F32).astype(BF16)
        part2[:, :, :, b * width:(b + 1) * width] = res.reshape(CORES, nc, rows, width)
    total = scatter_sum(part2, dbuf2, sbuf2, rbuf2, base3)
    h_mlp = DEEP_ALPHA * zall[blk].astype(F32) + total + vec(3)
    o = layer_norm(h_mlp, vec(4), vec(5))
    for b in range(nx):
        obuf[b] = o[:, b * width:(b + 1) * width]
    cps = [copy(obuf.at[x_at(d)], out_ref.at[x, blk], base4 + d, {'x': x_at(d)}) for d in range(1, nx)]
    for cp in cps:
        cp.start()
    out_ref[x, blk] = obuf[x]
    for d in range(1, nx):
        copy(obuf.at[x_at(d)], out_ref.at[x_at(-d), blk], base4 + d, {'x': x_at(d)}).wait_recv()
    share(lambda b: out_ref.at[:, b], base5)
    for cp in cps:
        cp.wait_send()


def tail(nx, ny, attn, hid, wo, vecs, wup, bup, wdn):
    nc = ny // CORES
    rows, total_width = hid.shape
    width = total_width // nx
    n_sem = 2 * nc + 2 * (2 * nc - 1) + nx + 1
    vm = pl.BlockSpec(memory_space=pltpu.VMEM)
    reduce_bufs = [pltpu.VMEM((CORES, nc, rows, total_width), BF16), pltpu.VMEM((nc, rows, total_width), BF16),
                   pltpu.VMEM((nc, rows, total_width), BF16), pltpu.VMEM((nc - 1, rows, total_width), BF16)]
    out = pl.pallas_call(
        functools.partial(tail_kernel, nx, ny),
        out_shape=jax.ShapeDtypeStruct((nx, ny, rows, width), BF16),
        in_specs=[vm] * 7,
        out_specs=vm,
        scratch_shapes=reduce_bufs + reduce_bufs + [
            pltpu.VMEM((ny, rows, total_width), BF16), pltpu.VMEM((nx, rows, width), BF16),
            pltpu.SemaphoreType.DMA((n_sem,)), pltpu.SemaphoreType.DMA((n_sem,))],
        compiler_params=pltpu.CompilerParams(collective_id=0, has_side_effects=True),
        name='tail',
    )(attn, hid, wo, vecs, wup, bup, wdn)
    return out.reshape(nx * ny * rows, width)


def apply_rotary(head_vec, positions):
    head_dim = head_vec.shape[-1]
    half_dim = head_dim // 2
    inv_freq = ROPE_BASE ** (-2.0 * jnp.arange(half_dim, dtype=jnp.float32) / head_dim)
    angles = positions.astype(jnp.float32)[:, None] * inv_freq[None, :]
    cos_table = jnp.cos(angles)[:, None, :]
    sin_table = jnp.sin(angles)[:, None, :]
    vec_wide = head_vec.astype(jnp.float32)
    lower_half = vec_wide[..., :half_dim]
    upper_half = vec_wide[..., half_dim:]
    return jnp.concatenate([lower_half * cos_table - upper_half * sin_table, upper_half * cos_table + lower_half * sin_table], axis=-1).astype(jnp.bfloat16)


def write_slot(cache, new_rows, lengths):
    slot_hit = jnp.arange(cache.shape[1])[None, :, None, None] == lengths[:, None, None, None]
    return jnp.where(slot_hit, new_rows[:, None], cache)


def attend(query_rot, k_full, v_full, lengths):
    head_dim = query_rot.shape[-1]
    scores = jnp.einsum('bhd,bshd->bhs', query_rot, k_full, preferred_element_type=jnp.float32) * (head_dim ** -0.5)
    slot_ok = jnp.arange(k_full.shape[1])[None, None, :] <= lengths[:, None, None]
    scores = jnp.where(slot_ok, scores, -1e30)
    attn_probs = jax.nn.softmax(scores, axis=-1).astype(jnp.bfloat16)
    attn_mixed = jnp.einsum('bhs,bshd->bhd', attn_probs, v_full, preferred_element_type=jnp.float32)
    return attn_mixed.astype(jnp.bfloat16).reshape(query_rot.shape[0], -1)


def solution(mesh):
    nx, ny = mesh.shape['x'], mesh.shape['y']
    cache_spec = P('dp', None, 'y', None)
    width_spec = P('x')
    in_specs = (P('dp', 'x'), P('x', 'y'), P('y'), P('y', 'x'), width_spec, width_spec, width_spec, P('x', None, 'y'), P(None, 'y'), P('y', 'x'), width_spec, width_spec, width_spec, cache_spec, cache_spec, P('dp'), P('dp'))
    out_specs = (P('dp', 'x'), cache_spec, cache_spec)

    def local_step(hidden, w_qkv, b_qkv, w_out, b_out, attn_gain, attn_shift, w_up, b_up, w_down, b_down, mlp_gain, mlp_shift, k_cache, v_cache, positions, lengths):
        row_count, width_local = hidden.shape
        local_heads, head_dim = k_cache.shape[2], k_cache.shape[3]
        x, y = lax.axis_index('x'), lax.axis_index('y')
        hidden_all = lax.all_gather(hidden, 'x', axis=1, tiled=True)
        wqkv_all = lax.all_gather(w_qkv, 'x', axis=0, tiled=True)
        vecs = jnp.stack([b_out, attn_gain, attn_shift, b_down, mlp_gain, mlp_shift, b_out, b_out])
        vecs = lax.all_gather(vecs, 'x')
        wo = lax.all_gather(w_out, 'x')
        wup = lax.all_gather(jnp.transpose(w_up, (1, 0, 2)), 'x')
        wdn = lax.all_gather(w_down, 'x')
        qkv_vals = (jnp.dot(hidden_all, wqkv_all, preferred_element_type=jnp.float32) + b_qkv.astype(jnp.float32)).astype(jnp.bfloat16)
        qkv_vals = qkv_vals.reshape(row_count, local_heads, 3, head_dim)
        query_rot = apply_rotary(qkv_vals[:, :, 0], positions)
        k_full = write_slot(k_cache, apply_rotary(qkv_vals[:, :, 1], positions), lengths)
        v_full = write_slot(v_cache, qkv_vals[:, :, 2], lengths)
        attn_out = attend(query_rot, k_full, v_full, lengths)
        per_x = row_count // nx
        per = per_x // ny
        blk = lax.rem(y, CORES) * (ny // CORES) + lax.div(y, CORES)
        attn_own = lax.dynamic_slice_in_dim(attn_out, x * per_x, per_x, 0)
        hid_own = lax.dynamic_slice_in_dim(hidden_all, x * per_x + blk * per, per, 0)
        result = tail(nx, ny, attn_own, hid_own, wo, vecs, wup, b_up, wdn)
        return result, k_full, v_full

    return jax.shard_map(local_step, mesh=mesh, in_specs=in_specs, out_specs=out_specs, check_vma=False)
```

time: 295 us -> 151 us (0.51)
  waiting for transfers between devices: 204 us -> 9.43 us
  Pallas kernels: 0 us -> 38.7 us
  blocking collectives: 17.3 us -> 37.2 us
  other arithmetic: 48 us -> 37.9 us
  local copies, waits for them, and re-layouts: 0.76 us -> 10.4 us
  matrix products: 7.27 us -> 2.62 us
    psum x4 -> x0, waiting for transfers between devices: 204 us -> none  [the longest x1 56.3 us: local_step(): proj_sum = lax.psum(proj_part, 'y')]
    pallas_call x0 -> x1, Pallas kernels: none -> 38.7 us  [tail(): pl.pallas_call(functools.partial(tail_kernel, nx, ny), out_shape=jax.Shap...]
    all_gather x0 -> x3, blocking collectives: none -> 37.2 us  [the longest x1 15.8 us: local_step(): wqkv_all = lax.all_gather(w_qkv, 'x', axis=0, tiled=True)]
    psum x2 -> x0, blocking collectives: 17.3 us -> none  [sharded_norm(): moments = lax.psum(moments, 'x')]
    all_gather x0 -> x3, waiting for transfers between devices: none -> 7.92 us  [the longest x1 7.9 us: local_step(): wup = lax.all_gather(jnp.transpose(w_up, (1, 0, 2)), 'x')]
    convert_element_type x10 -> x0, other arithmetic: 4.88 us -> none  [the longest x2 3.58 us: sharded_norm(): (scaled * gain.astype(jnp.float32) + shift.astype(jnp.float32)).astype(jn...]
    dot_general x4 -> x1, matrix products: 7.27 us -> 2.62 us  [local_step(): jnp.dot(hidden_all, wqkv_all, preferred_element_type=jnp.float32)]
    unnamed x23 -> x4, local copies, waits for them, and re-layouts: 0.47 us -> 4.91 us
  transfers between devices with their start and end apart: 4 -> 3, of which waited for: 4 -> 1; matrix products, arithmetic and copies ran while one was open for 1% -> 33% of each run, Pallas kernels for 0% -> 0%
where the time goes in v1:
time: 151 us; the launch traced here: 150 us
  Pallas kernels  38.7 us (26%)
  other arithmetic  37.9 us (25%)
  blocking collectives  37.2 us (25%)
  between operations  13.9 us (9%)
  local copies, waits for them, and re-layouts  10.4 us (7%)
  waiting for transfers between devices  9.43 us (6%)
  matrix products  2.62 us (2%)
    pallas_call x1, Pallas kernels, tail(): pl.pallas_call(functools.partial(tail_kernel, nx, ny), out_shape=jax.Shap...  38.7 us
    dot_general x1, other arithmetic, attend(): jnp.einsum('bhs,bshd->bhd', attn_probs, v_full, preferred_element_type=jn...  17.7 us
    unnamed x2, other arithmetic  17 us
    all_gather x1, blocking collectives, local_step(): wqkv_all = lax.all_gather(w_qkv, 'x', axis=0, tiled=True)  15.8 us
    all_gather x1, blocking collectives, local_step(): wo = lax.all_gather(w_out, 'x')  12.5 us
    all_gather x1, blocking collectives, local_step(): vecs = lax.all_gather(vecs, 'x')  8.98 us
    all_gather x1, waiting for transfers between devices, local_step(): wup = lax.all_gather(jnp.transpose(w_up, (1, 0, 2)), 'x')  7.9 us
    unnamed x4, local copies, waits for them, and re-layouts  4.91 us
  transfers between devices with their start and end apart: 3, of which 1 were waited for; matrix products, arithmetic and copies ran while one was open for 33% of the time, Pallas kernels for 0%

profile of v1, /device:TPU:97, one launch (start us, length us, event | category | flops | bytes accessed | tf_op | source)
XLA Modules:
  0.0 150.3 jit_solution(12443782526141272909)
XLA Ops:
  7.2 0.1 all-gather.8.cloned.1.call-start
  7.2 0.7 all-gather.8.cloned.1.call-update
  8.0 0.1 all-gather.12.cloned.1.call-start
  8.0 0.7 all-gather.12.cloned.1.call-update
  8.8 0.1 all-gather.10.cloned.1.call-start
  8.9 1.9 %copy.61 = bf16[256,2,512]{2,0,1:T(8,128)(2,1)} copy(bf16[256,2,512]{2,1,0:T(2,128)(2,1)} %param.24) | data formatting | bytes 1048576 | tf_op args[7]
  10.7 0.1 all-gather.10.cloned.1.call-update
  10.8 15.8 %all_gather.31 = bf16[1024,384]{1,0:T(8,128)(2,1)S(1)} all-gather(bf16[256,384]{1,0:T(8,128)(2,1)} %param.18), channel_id=1, replica_groups=mesh['dp'=1,'x'=4,'y'=8] {'x'}, dimensions={0}, use_global_device_ids=true | all-gather | bytes 983040 | tf_op jit(solution)/shard_map/all_gather | solution.py:193
  26.6 0.7 convert_element_type.34
  27.3 0.7 convert_element_type.38
  28.0 0.8 iota_compare_fusion.1
  28.7 12.5 %all-gather = bf16[512,256]{1,0:T(8,128)(2,1)} all-gather(bf16[128,256]{1,0:T(8,128)(2,1)} %param.20), channel_id=2, replica_groups=mesh['dp'=1,'x'=4,'y'=8] {'x'}, dimensions={0}, use_global_device_ids=true | all-gather | bytes 327680 | tf_op jit(solution)/shard_map/all_gather | solution.py:196
  41.2 0.7 stack.23
  41.9 0.7 stack.24
  42.5 0.7 stack.25
  43.2 0.7 stack.26
  43.8 0.7 stack.27
  44.5 0.7 stack.28
  45.2 9.0 %all-gather.1 = bf16[32,256]{1,0:T(8,128)(2,1)} all-gather(bf16[8,256]{1,0:T(8,128)(2,1)S(1)} %stack.29), channel_id=3, replica_groups=mesh['dp'=1,'x'=4,'y'=8] {'x'}, dimensions={0}, use_global_device_ids=true | all-gather | bytes 20480 | tf_op jit(solution)/shard_map/all_gather | solution.py:195
  54.2 0.5 multiply_cosine_fusion
  54.7 0.0 all-gather.8.cloned.1.call-done
  54.7 2.6 %add_convert_fusion = bf16[1024,384]{0,1:T(8,128)(2,1)S(1)} fusion(bf16[1024,1024]{1,0:T(8,128)(2,1)} %all-gather.8.cloned.1.call-done, bf16[1024,384]{1,0:T(8,128)(2,1)S(1)} %all_gather.31, f32[384]{0:T(512)S(1)} %convert_element_type.34), kind=kOutput, calls=%fused_computation.6 | convolution fusion | flops 806092800 | bytes 3671552 | tf_op jit(solution)/shard_map/dot_general | solution.py:199
  57.3 0.1 slice_bitcast_fusion
  57.4 0.1 subtract_convert_fusion
  57.6 0.1 maximum_convert_fusion
  57.7 16.9 %multiply_reduce_fusion.1 = (f32[1024,2,64]{0,1,2:T(2,128)S(1)}, bf16[1024,64,2,64]{0,3,2,1:T(8,128)(2,1)}) fusion(f32[1024,2,64]{0,2,1:T(8,128)S(1)} %get-tuple-element.20, bf16[1024,64,2,64]{0,3,2,1:T(8,128)(2,1)} %param.30, bf16[1024,2,64]{0,2,1:T(8,128)(2,1)S(1)} %get-tuple-element.21, pred[1024,64]{0,1:T(8,128)(4,1)S(1)} %get-tuple-element.19), kind=kLoop, calls=%fused_computation.3 | loop fusion | flops 33423360 | bytes 34930688
  74.6 0.3 fusion.6
  74.9 0.4 copy.50
  75.4 17.7 %multiply_reduce_fusion = (bf16[1024,2,64]{0,2,1:T(8,128)(2,1)S(1)}, bf16[1024,64,2,64]{0,3,2,1:T(8,128)(2,1)}) fusion(f32[1024,2,64]{0,1,2:T(2,128)S(1)} %copy.50, bf16[1024,64,2,64]{0,3,2,1:T(8,128)(2,1)} %param.31, bf16[1024,2,64]{0,2,1:T(8,128)(2,1)S(1)} %get-tuple-element.7, pred[1024,64]{0,1:T(8,128)(4,1)S(1)} %get-tuple-element.19), kind=kLoop, calls=%fused_computation.2 | loop fusion | flops 33423360 | bytes 34668544 | tf_op jit(solution)/shard_map/bhs,bshd->bhd/dot_general | solution.py:177
  93.0 0.8 copy.48.attn_ref
  93.8 1.5 constant_dynamic-slice_fusion.hid_ref
  95.3 0.0 all-gather.12.cloned.1.call-done
  95.3 7.9 %all-gather.10.cloned.1.call-done = bf16[8,256,512]{2,1,0:T(8,128)(2,1)} async-done(((bf16[2,256,512]{2,1,0:T(8,128)(2,1)}), bf16[8,256,512]{2,1,0:T(8,128)(2,1)}) %all-gather.10.cloned.1.call-update) | async-done | bytes 2097168 | tf_op jit(solution)/shard_map/all_gather | solution.py:197
  103.2 38.7 %tail.1 = bf16[4,8,32,256]{3,2,1,0:T(8,128)(2,1)} custom-call(bf16[256,128]{1,0:T(8,128)(2,1)} %copy.48.attn_ref, bf16[32,1024]{1,0:T(8,128)(2,1)} %constant_dynamic-slice_fusion.hid_ref, bf16[4,128,256]{2,1,0:T(8,128)(2,1)} %bitcast.34, bf16[4,8,256]{2,1,0:T(8,128)(2,1)} %bitcast.37, bf16[4,2,256,512]{3,2,1,0:T(8,128)(2,1)} %bitcast.30, ...), custom_call_target="tpu_custom_call" | custom-call | tf_op jit(solution)/shard_map/tail/pallas_call | solution.py:139
  141.9 1.9 %copy.63 = bf16[1024,256]{1,0:T(8,128)(2,1)} copy(bf16[1024,256]{1,0:T(8,128)(2,1)} %bitcast.31) | data formatting | bytes 1048576
  (3 shorter events, 0.1 us)
Async XLA Ops:
  7.2 47.5 %all-gather.8.cloned.1.call-start = ((), (), s32[]{:S(2)}) async-start(), calls=%async_computation | async-start | bytes 2621440 | tf_op jit(solution)/shard_map/all_gather | solution.py:192
  8.0 87.3 %all-gather.12.cloned.1.call-start = ((), (), s32[]{:S(2)}) async-start(), calls=%async_computation.2 | async-start | bytes 1310720 | tf_op jit(solution)/shard_map/all_gather | solution.py:198
  8.8 94.4 %all-gather.10.cloned.1.call-start = ((), (), s32[]{:S(2)}) async-start(), calls=%async_computation.1 | async-start | bytes 2621440 | tf_op jit(solution)/shard_map/all_gather | solution.py:197
Sparse Core Ops, SparseCore 0:
  9.6 38.2 all-gather.7
  49.4 21.1 all-gather.11
  72.7 30.4 all-gather.9

commit v2 on v1

--- a/solution.py
+++ b/solution.py
@@ -150,6 +150,86 @@
     return out.reshape(nx * ny * rows, width)
 
 
+def cache_kernel(n_blocks, k_ref, v_ref, kn_ref, vn_ref, q_ref, lens_ref, lane_ref, ko_ref, vo_ref, attn_ref,
+                 qs, sc, acc):
+    step = pl.program_id(0)
+    slots, heads, dim, _ = k_ref.shape
+    own = q_ref.shape[2]
+    cols = pl.ds(pl.multiple_of(lax.axis_index('x') * own, own), own)
+    total_slots = n_blocks * slots
+
+    @pl.when(step == 0)
+    def _():
+        qs[...] = q_ref[...].astype(F32)
+        acc[...] = jnp.zeros_like(acc)
+
+    def write(src, new, dst, first):
+        for s in range(slots):
+            hit = lane_ref[...] == (first + s).astype(F32).astype(BF16)
+            for h in range(heads):
+                for t in range(dim // 16):
+                    part = pl.ds(t * 16, 16)
+                    dst[s, h, part, :] = jnp.where(hit, new[h, part, :], src[s, h, part, :])
+
+    @pl.when(step < n_blocks)
+    def _():
+        first = step * slots
+        write(k_ref, kn_ref, ko_ref, first)
+        for s in range(slots):
+            for h in range(heads):
+                sc[h, pl.ds(first + s, 1), :] = jnp.sum(
+                    ko_ref[s, h, :, cols].astype(F32) * qs[h], axis=0, keepdims=True)
+
+    @pl.when(step == n_blocks - 1)
+    def _():
+        slot = lax.broadcasted_iota(jnp.int32, (total_slots, own), 0)
+        ok = slot <= lens_ref[:, cols]
+        for h in range(heads):
+            s = jnp.where(ok, sc[h] * (dim ** -0.5), -1e30)
+            e = jnp.exp(s - jnp.max(s, axis=0, keepdims=True))
+            p = e / jnp.sum(e, axis=0, keepdims=True)
+            sc[h] = p.astype(BF16).astype(F32)
+
+    @pl.when(step >= n_blocks)
+    def _():
+        first = (step - n_blocks) * slots
+        write(v_ref, vn_ref, vo_ref, first)
+        for h in range(heads):
+            a = acc[h]
+            for s in range(slots):
+                a = a + vo_ref[s, h, :, cols].astype(F32) * sc[h, pl.ds(first + s, 1), :]
+            acc[h] = a
+
+    @pl.when(step == 2 * n_blocks - 1)
+    def _():
+        attn_ref[...] = acc[...].reshape(heads * dim, own).T.astype(BF16)
+
+
+def cache_step(k_t, v_t, k_new, v_new, q_own, lengths, slots=4):
+    total_slots, heads, dim, rows = k_t.shape
+    own = q_own.shape[2]
+    n = total_slots // slots
+    blk = (slots, heads, dim, rows)
+    lens = lengths.reshape(1, rows)
+    lane = jnp.broadcast_to(lengths.astype(BF16)[None], (16, rows))
+    k_spec = pl.BlockSpec(blk, lambda i: (jnp.minimum(i, n - 1), 0, 0, 0))
+    v_spec = pl.BlockSpec(blk, lambda i: (jnp.maximum(i - n, 0), 0, 0, 0))
+    whole = pl.BlockSpec(memory_space=pltpu.VMEM)
+    shape = jax.ShapeDtypeStruct(k_t.shape, k_t.dtype)
+    size = 4 * k_t.size * 2
+    return pl.pallas_call(
+        functools.partial(cache_kernel, n),
+        grid=(2 * n,),
+        out_shape=(shape, shape, jax.ShapeDtypeStruct((own, heads * dim), BF16)),
+        in_specs=[k_spec, v_spec] + [whole] * 5,
+        out_specs=(k_spec, v_spec, whole),
+        scratch_shapes=[pltpu.VMEM((heads, dim, own), F32), pltpu.VMEM((heads, total_slots, own), F32),
+                        pltpu.VMEM((heads, dim, own), F32)],
+        cost_estimate=pl.CostEstimate(flops=40 * k_t.size, bytes_accessed=size, transcendentals=0),
+        name='cache_step',
+    )(k_t, v_t, k_new, v_new, q_own, lens, lane)
+
+
 def apply_rotary(head_vec, positions):
     head_dim = head_vec.shape[-1]
     half_dim = head_dim // 2
@@ -161,21 +241,6 @@
     lower_half = vec_wide[..., :half_dim]
     upper_half = vec_wide[..., half_dim:]
     return jnp.concatenate([lower_half * cos_table - upper_half * sin_table, upper_half * cos_table + lower_half * sin_table], axis=-1).astype(jnp.bfloat16)
-
-
-def write_slot(cache, new_rows, lengths):
-    slot_hit = jnp.arange(cache.shape[1])[None, :, None, None] == lengths[:, None, None, None]
-    return jnp.where(slot_hit, new_rows[:, None], cache)
-
-
-def attend(query_rot, k_full, v_full, lengths):
-    head_dim = query_rot.shape[-1]
-    scores = jnp.einsum('bhd,bshd->bhs', query_rot, k_full, preferred_element_type=jnp.float32) * (head_dim ** -0.5)
-    slot_ok = jnp.arange(k_full.shape[1])[None, None, :] <= lengths[:, None, None]
-    scores = jnp.where(slot_ok, scores, -1e30)
-    attn_probs = jax.nn.softmax(scores, axis=-1).astype(jnp.bfloat16)
-    attn_mixed = jnp.einsum('bhs,bshd->bhd', attn_probs, v_full, preferred_element_type=jnp.float32)
-    return attn_mixed.astype(jnp.bfloat16).reshape(query_rot.shape[0], -1)
 
 
 def solution(mesh):
@@ -198,14 +263,17 @@
         wdn = lax.all_gather(w_down, 'x')
         qkv_vals = (jnp.dot(hidden_all, wqkv_all, preferred_element_type=jnp.float32) + b_qkv.astype(jnp.float32)).astype(jnp.bfloat16)
         qkv_vals = qkv_vals.reshape(row_count, local_heads, 3, head_dim)
-        query_rot = apply_rotary(qkv_vals[:, :, 0], positions)
-        k_full = write_slot(k_cache, apply_rotary(qkv_vals[:, :, 1], positions), lengths)
-        v_full = write_slot(v_cache, qkv_vals[:, :, 2], lengths)
-        attn_out = attend(query_rot, k_full, v_full, lengths)
+        heads_first = lambda v: jnp.transpose(v, (1, 2, 0))
         per_x = row_count // nx
+        q_t = heads_first(apply_rotary(qkv_vals[:, :, 0], positions))
+        q_own = lax.dynamic_slice_in_dim(q_t, x * per_x, per_x, 2)
+        k_new = heads_first(apply_rotary(qkv_vals[:, :, 1], positions))
+        v_new = heads_first(qkv_vals[:, :, 2])
+        k_t, v_t = jnp.transpose(k_cache, (1, 2, 3, 0)), jnp.transpose(v_cache, (1, 2, 3, 0))
+        k_t, v_t, attn_own = cache_step(k_t, v_t, k_new, v_new, q_own, lengths)
+        k_full, v_full = jnp.transpose(k_t, (3, 0, 1, 2)), jnp.transpose(v_t, (3, 0, 1, 2))
         per = per_x // ny
         blk = lax.rem(y, CORES) * (ny // CORES) + lax.div(y, CORES)
-        attn_own = lax.dynamic_slice_in_dim(attn_out, x * per_x, per_x, 0)
         hid_own = lax.dynamic_slice_in_dim(hidden_all, x * per_x + blk * per, per, 0)
         result = tail(nx, ny, attn_own, hid_own, wo, vecs, wup, b_up, wdn)
         return result, k_full, v_full

time: 151 us -> 153 us (1.013)
  Pallas kernels: 38.7 us -> 75.6 us
  other arithmetic: 37.9 us -> 2.84 us
  local copies, waits for them, and re-layouts: 10.4 us -> 5.93 us
  waiting for transfers between devices: 9.43 us -> 12.7 us
    pallas_call x0 -> x1, Pallas kernels: none -> 36.9 us  [cache_step(): pl.pallas_call(functools.partial(cache_kernel, n), grid=(2 * n,), out_sha...]
    dot_general x1 -> x0, other arithmetic: 17.7 us -> none  [attend(): jnp.einsum('bhs,bshd->bhd', attn_probs, v_full, preferred_element_type=jn...]
    unnamed x2 -> x0, other arithmetic: 17 us -> none
    another operation x7, local copies, waits for them, and re-layouts: 3.98 us -> 0.06 us  [local_step(): jnp.stack([b_out, attn_gain, attn_shift, b_down, mlp_gain, mlp_shift, b_o...]
    all_gather x1, waiting for transfers between devices: 7.9 us -> 11.2 us  [local_step(): wup = lax.all_gather(jnp.transpose(w_up, (1, 0, 2)), 'x')]
    all_gather x1, blocking collectives: 8.98 us -> 11.6 us  [local_step(): vecs = lax.all_gather(vecs, 'x')]
    unnamed x4 -> x24, local copies, waits for them, and re-layouts: 4.91 us -> 3.81 us
  transfers between devices with their start and end apart: 3 -> 3, of which waited for: 1 -> 1; matrix products, arithmetic and copies ran while one was open for 33% -> 6% of each run, Pallas kernels for 0% -> 24%
where the time goes in v2:
time: 153 us; the launch traced here: 152 us
  Pallas kernels  75.6 us (49%)
  blocking collectives  37.5 us (25%)
  between operations  14.1 us (9%)
  waiting for transfers between devices  12.7 us (8%)
  local copies, waits for them, and re-layouts  5.93 us (4%)
  other arithmetic  2.84 us (2%)
  matrix products  2.61 us (2%)
    pallas_call x1, Pallas kernels, tail(): pl.pallas_call(functools.partial(tail_kernel, nx, ny), out_shape=jax.Shap...  38.7 us
    pallas_call x1, Pallas kernels, cache_step(): pl.pallas_call(functools.partial(cache_kernel, n), grid=(2 * n,), out_sha...  36.9 us
    all_gather x1, blocking collectives, local_step(): wqkv_all = lax.all_gather(w_qkv, 'x', axis=0, tiled=True)  14.4 us
    all_gather x1, blocking collectives, local_step(): vecs = lax.all_gather(vecs, 'x')  11.6 us
    all_gather x1, blocking collectives, local_step(): wo = lax.all_gather(w_out, 'x')  11.5 us
    all_gather x1, waiting for transfers between devices, local_step(): wup = lax.all_gather(jnp.transpose(w_up, (1, 0, 2)), 'x')  11.2 us
    unnamed x24, local copies, waits for them, and re-layouts  3.81 us
  transfers between devices with their start and end apart: 3, of which 1 were waited for; matrix products, arithmetic and copies ran while one was open for 6% of the time, Pallas kernels for 24%

profile of v2, /device:TPU:97, one launch (start us, length us, event | category | flops | bytes accessed | tf_op | source)
XLA Modules:
  0.0 151.5 jit_solution(7384299872649403010)
XLA Ops:
  7.2 0.0 copy-start.4
  7.2 0.0 copy-start.3
  7.2 0.0 copy-start.2
  7.2 0.0 copy-start.5
  7.2 0.0 copy-start.6
  7.2 0.0 copy-start.7
  7.2 0.0 copy-start.8
  7.3 0.0 copy-start.9
  7.3 0.0 copy-start.10
  7.3 0.0 copy-start.1
  7.3 0.0 copy-start
  7.3 0.1 all-gather.8.cloned.1.call-start
  7.4 0.7 all-gather.8.cloned.1.call-update
  8.1 0.1 all-gather.12.cloned.1.call-start
  8.2 0.7 all-gather.12.cloned.1.call-update
  8.9 0.1 all-gather.10.cloned.1.call-start
  9.0 1.9 %copy.33 = bf16[256,2,512]{2,0,1:T(8,128)(2,1)} copy(bf16[256,2,512]{2,1,0:T(2,128)(2,1)} %param.24) | data formatting | bytes 1048576 | tf_op args[7]
  10.9 0.1 all-gather.10.cloned.1.call-update
  10.9 0.0 copy-done.4
  11.0 0.0 copy-done.3
  11.0 0.0 copy-done.2
  11.0 0.0 copy-done.5
  11.0 0.0 copy-done.6
  11.0 0.0 copy-done.7
  11.1 0.0 copy-done.8
  11.1 0.0 copy-done.9
  11.1 0.0 copy-done.10
  11.2 11.6 %all-gather.1 = bf16[32,256]{1,0:T(8,128)(2,1)} all-gather(bf16[8,256]{1,0:T(8,128)(2,1)S(1)} %stack.29), channel_id=3, replica_groups=mesh['dp'=1,'x'=4,'y'=8] {'x'}, dimensions={0}, use_global_device_ids=true | all-gather | bytes 20480 | tf_op jit(solution)/shard_map/all_gather | solution.py:260
  22.8 0.0 copy-done.1
  22.8 11.5 %all-gather = bf16[512,256]{1,0:T(8,128)(2,1)} all-gather(bf16[128,256]{1,0:T(8,128)(2,1)S(1)} %copy-done.1), channel_id=2, replica_groups=mesh['dp'=1,'x'=4,'y'=8] {'x'}, dimensions={0}, use_global_device_ids=true | all-gather | bytes 327680 | tf_op jit(solution)/shard_map/all_gather | solution.py:261
  34.3 0.5 multiply_cosine_fusion
  34.8 0.0 copy-done
  34.8 14.4 %all_gather.31 = bf16[1024,384]{1,0:T(8,128)(2,1)S(1)} all-gather(bf16[256,384]{1,0:T(8,128)(2,1)S(1)} %copy-done), channel_id=1, replica_groups=mesh['dp'=1,'x'=4,'y'=8] {'x'}, dimensions={0}, use_global_device_ids=true | all-gather | bytes 983040 | tf_op jit(solution)/shard_map/all_gather | solution.py:258
  49.2 0.0 all-gather.8.cloned.1.call-done
  49.2 2.6 %add_convert_fusion = bf16[1024,384]{0,1:T(8,128)(2,1)S(1)} fusion(bf16[1024,1024]{1,0:T(8,128)(2,1)} %all-gather.8.cloned.1.call-done, bf16[1024,384]{1,0:T(8,128)(2,1)S(1)} %all_gather.31, f32[384]{0:T(512)S(1)} %convert_element_type.27), kind=kOutput, calls=%fused_computation | convolution fusion | flops 806092800 | bytes 3671552 | tf_op jit(solution)/shard_map/dot_general | solution.py:264
  51.9 0.8 fusion
  52.7 0.1 add_convert_fusion.1
  52.8 0.6 fusion.3.q_ref
  53.4 0.7 maximum_bitcast_fusion.kn_ref
  54.1 0.6 broadcast_in_dim.2.lane_ref
  54.7 36.9 %cache_step.1 = (bf16[64,2,64,1024]{3,2,1,0:T(8,128)(2,1)}, bf16[64,2,64,1024]{3,2,1,0:T(8,128)(2,1)}, bf16[256,128]{1,0:T(8,128)(2,1)}) custom-call(bf16[64,2,64,1024]{3,2,1,0:T(8,128)(2,1)} %bitcast.40, bf16[64,2,64,1024]{3,2,1,0:T(8,128)(2,1)} %bitcast.41, bf16[2,64,1024]{2,1,0:T(8,128)(2,1)} %maximum_bitcast_fusion.kn_ref, ...), custom_call_target="tpu_custom_call" | custom-call | flops 335544320 | bytes 67108864 | tf_op jit(solution)/shard_map/cache_step/pallas_call | solution.py:220
  91.7 1.5 constant_dynamic-slice_fusion.hid_ref
  93.1 0.0 all-gather.12.cloned.1.call-done
  93.1 11.2 %all-gather.10.cloned.1.call-done = bf16[8,256,512]{2,1,0:T(8,128)(2,1)} async-done(((bf16[2,256,512]{2,1,0:T(8,128)(2,1)}), bf16[8,256,512]{2,1,0:T(8,128)(2,1)}) %all-gather.10.cloned.1.call-update) | async-done | bytes 2097168 | tf_op jit(solution)/shard_map/all_gather | solution.py:262
  104.4 38.7 %tail.1 = bf16[4,8,32,256]{3,2,1,0:T(8,128)(2,1)} custom-call(bf16[256,128]{1,0:T(8,128)(2,1)} %get-tuple-element.6.attn_ref, bf16[32,1024]{1,0:T(8,128)(2,1)} %constant_dynamic-slice_fusion.hid_ref, bf16[4,128,256]{2,1,0:T(8,128)(2,1)} %bitcast.46, bf16[4,8,256]{2,1,0:T(8,128)(2,1)} %bitcast.48, bf16[4,2,256,512]{3,2,1,0:T(8,128)(2,1)} %bitcast.42, ...), custom_call_target="tpu_custom_call" | custom-call | tf_op jit(solution)/shard_map/tail/pallas_call | solution.py:139
  143.1 1.9 %copy.35 = bf16[1024,256]{1,0:T(8,128)(2,1)} copy(bf16[1024,256]{1,0:T(8,128)(2,1)} %bitcast.43) | data formatting | bytes 1048576
  (11 shorter events, 0.1 us)
Async XLA Ops:
  7.2 3.8 %copy-start.4 = (bf16[384]{0:T(512)(128)(2,1)S(1)}, bf16[384]{0:T(512)(128)(2,1)}, u32[]{:S(2)}) copy-start(bf16[384]{0:T(512)(128)(2,1)} %param.19) | copy-start | bytes 2308
  7.2 3.8 %copy-start.3 = (s32[1024]{0:T(1024)S(1)}, s32[1024]{0:T(1024)}, u32[]{:S(2)}) copy-start(s32[1024]{0:T(1024)} %param.32) | copy-start | bytes 12292
  7.2 3.8 %copy-start.2 = (s32[1024]{0:T(1024)S(1)}, s32[1024]{0:T(1024)}, u32[]{:S(2)}) copy-start(s32[1024]{0:T(1024)} %param.33) | copy-start | bytes 12292
  7.2 3.8 %copy-start.5 = (bf16[256]{0:T(256)(128)(2,1)S(1)}, bf16[256]{0:T(256)(128)(2,1)}, u32[]{:S(2)}) copy-start(bf16[256]{0:T(256)(128)(2,1)} %param.21) | copy-start | bytes 1540
  7.2 3.8 %copy-start.6 = (bf16[256]{0:T(256)(128)(2,1)S(1)}, bf16[256]{0:T(256)(128)(2,1)}, u32[]{:S(2)}) copy-start(bf16[256]{0:T(256)(128)(2,1)} %param.22) | copy-start | bytes 1540
  7.2 3.8 %copy-start.7 = (bf16[256]{0:T(256)(128)(2,1)S(1)}, bf16[256]{0:T(256)(128)(2,1)}, u32[]{:S(2)}) copy-start(bf16[256]{0:T(256)(128)(2,1)} %param.23) | copy-start | bytes 1540
  7.2 3.8 %copy-start.8 = (bf16[256]{0:T(256)(128)(2,1)S(1)}, bf16[256]{0:T(256)(128)(2,1)}, u32[]{:S(2)}) copy-start(bf16[256]{0:T(256)(128)(2,1)} %param.27) | copy-start | bytes 1540
  7.3 3.8 %copy-start.9 = (bf16[256]{0:T(256)(128)(2,1)S(1)}, bf16[256]{0:T(256)(128)(2,1)}, u32[]{:S(2)}) copy-start(bf16[256]{0:T(256)(128)(2,1)} %param.28) | copy-start | bytes 1540
  7.3 3.8 %copy-start.10 = (bf16[256]{0:T(256)(128)(2,1)S(1)}, bf16[256]{0:T(256)(128)(2,1)}, u32[]{:S(2)}) copy-start(bf16[256]{0:T(256)(128)(2,1)} %param.29) | copy-start | bytes 1540
  7.3 15.5 %copy-start.1 = (bf16[128,256]{1,0:T(8,128)(2,1)S(1)}, bf16[128,256]{1,0:T(8,128)(2,1)}, u32[]{:S(2)}) copy-start(bf16[128,256]{1,0:T(8,128)(2,1)} %param.20) | copy-start | bytes 196612
  7.3 27.5 %copy-start = (bf16[256,384]{1,0:T(8,128)(2,1)S(1)}, bf16[256,384]{1,0:T(8,128)(2,1)}, u32[]{:S(2)}) copy-start(bf16[256,384]{1,0:T(8,128)(2,1)} %param.18) | copy-start | bytes 589828
  7.3 41.9 %all-gather.8.cloned.1.call-start = ((), (), s32[]{:S(2)}) async-start(), calls=%async_computation | async-start | bytes 2621440 | tf_op jit(solution)/shard_map/all_gather | solution.py:257
  8.1 85.0 %all-gather.12.cloned.1.call-start = ((), (), s32[]{:S(2)}) async-start(), calls=%async_computation.2 | async-start | bytes 1310720 | tf_op jit(solution)/shard_map/all_gather | solution.py:263
  8.9 95.5 %all-gather.10.cloned.1.call-start = ((), (), s32[]{:S(2)}) async-start(), calls=%async_computation.1 | async-start | bytes 2621440 | tf_op jit(solution)/shard_map/all_gather | solution.py:262
Sparse Core Ops, SparseCore 0:
  9.7 37.5 all-gather.7
  48.8 22.8 all-gather.11
  73.9 30.4 all-gather.9

commit v3 on v2

--- a/solution.py
+++ b/solution.py
@@ -23,15 +23,16 @@
     return (cent * lax.rsqrt(var_row + LN_EPS) * gain + shift).astype(BF16)
 
 
-def tail_kernel(nx, ny, attn_ref, hid_ref, wo_ref, vec_ref, wup_ref, bup_ref, wdn_ref, out_ref,
-                part1, dbuf1, sbuf1, rbuf1, part2, dbuf2, sbuf2, rbuf2, zall, obuf, send, recv):
+def tail_kernel(nx, ny, attn_ref, hid_ref, vec_ref, bup_ref, *refs):
+    wo_ref, wup_ref, wdn_ref = refs[:nx], refs[nx:2 * nx], refs[2 * nx:3 * nx]
+    (out_ref, part1, dbuf1, sbuf1, rbuf1, part2, dbuf2, sbuf2, rbuf2, zall, obuf, send, recv) = refs[3 * nx:]
     nc = ny // CORES
     x, y = lax.axis_index('x'), lax.axis_index('y')
     core, chip = lax.rem(y, CORES), lax.div(y, CORES)
     partner = {'y': chip * CORES + (1 - core)}
     blk = core * nc + chip
     rows = hid_ref.shape[0]
-    width = vec_ref.shape[2]
+    width = hid_ref.shape[1] // nx
 
     def chip_at(d):
         return lax.rem(chip + d + nc, nc)
@@ -55,7 +56,10 @@
     pl.semaphore_wait(barrier, nc + nx - 1)
 
     def vec(i):
-        return jnp.concatenate([vec_ref[b, i:i + 1, :] for b in range(nx)], axis=1).astype(F32)
+        return vec_ref[i:i + 1, :]
+
+    def x_cols(d):
+        return pl.ds(pl.multiple_of(x_at(d) * width, width), width)
 
     def scatter_sum(part, dbuf, sbuf, rbuf, base):
         cp = copy(part.at[1 - core], dbuf, base, partner)
@@ -93,25 +97,24 @@
     base1, base2, base3, base4, base5 = 0, nc, nc + per, 2 * nc + per, 2 * nc + per + nx
 
     for b in range(nx):
-        res = jnp.dot(attn_ref[...], wo_ref[b], preferred_element_type=F32).astype(BF16)
-        part1[:, :, :, b * width:(b + 1) * width] = res.reshape(CORES, nc, rows, width)
+        res = jnp.dot(attn_ref[...], wo_ref[b][...], preferred_element_type=F32).astype(BF16)
+        part1[:, :, :, x_cols(b)] = res.reshape(CORES, nc, rows, width)
     total = scatter_sum(part1, dbuf1, sbuf1, rbuf1, base1)
     h_attn = DEEP_ALPHA * hid_ref[...].astype(F32) + total + vec(0)
     z_own = layer_norm(h_attn, vec(1), vec(2))
     zall[blk] = z_own
     share(lambda b: zall.at[b], base2)
 
-    z = zall[...].reshape(ny * rows, nx * width)
     gate = bup_ref[0:1, :].astype(F32)
     val = bup_ref[1:2, :].astype(F32)
     for b in range(nx):
-        zb = z[:, b * width:(b + 1) * width]
-        gate = gate + jnp.dot(zb, wup_ref[b, 0], preferred_element_type=F32)
-        val = val + jnp.dot(zb, wup_ref[b, 1], preferred_element_type=F32)
+        zb = zall[:, :, x_cols(b)].reshape(ny * rows, width)
+        gate = gate + jnp.dot(zb, wup_ref[b][0], preferred_element_type=F32)
+        val = val + jnp.dot(zb, wup_ref[b][1], preferred_element_type=F32)
     g = (jax.nn.gelu(gate, approximate=True) * val).astype(BF16)
     for b in range(nx):
-        res = jnp.dot(g, wdn_ref[b], preferred_element_type=F32).astype(BF16)
-        part2[:, :, :, b * width:(b + 1) * width] = res.reshape(CORES, nc, rows, width)
+        res = jnp.dot(g, wdn_ref[b][...], preferred_element_type=F32).astype(BF16)
+        part2[:, :, :, x_cols(b)] = res.reshape(CORES, nc, rows, width)
     total = scatter_sum(part2, dbuf2, sbuf2, rbuf2, base3)
     h_mlp = DEEP_ALPHA * zall[blk].astype(F32) + total + vec(3)
     o = layer_norm(h_mlp, vec(4), vec(5))
@@ -139,14 +142,14 @@
     out = pl.pallas_call(
         functools.partial(tail_kernel, nx, ny),
         out_shape=jax.ShapeDtypeStruct((nx, ny, rows, width), BF16),
-        in_specs=[vm] * 7,
+        in_specs=[vm] * (4 + 3 * nx),
         out_specs=vm,
         scratch_shapes=reduce_bufs + reduce_bufs + [
             pltpu.VMEM((ny, rows, total_width), BF16), pltpu.VMEM((nx, rows, width), BF16),
             pltpu.SemaphoreType.DMA((n_sem,)), pltpu.SemaphoreType.DMA((n_sem,))],
         compiler_params=pltpu.CompilerParams(collective_id=0, has_side_effects=True),
         name='tail',
-    )(attn, hid, wo, vecs, wup, bup, wdn)
+    )(attn, hid, vecs, bup, *wo, *wup, *wdn)
     return out.reshape(nx * ny * rows, width)
 
 
@@ -230,17 +233,212 @@
     )(k_t, v_t, k_new, v_new, q_own, lens, lane)
 
 
-def apply_rotary(head_vec, positions):
-    head_dim = head_vec.shape[-1]
-    half_dim = head_dim // 2
-    inv_freq = ROPE_BASE ** (-2.0 * jnp.arange(half_dim, dtype=jnp.float32) / head_dim)
-    angles = positions.astype(jnp.float32)[:, None] * inv_freq[None, :]
-    cos_table = jnp.cos(angles)[:, None, :]
-    sin_table = jnp.sin(angles)[:, None, :]
-    vec_wide = head_vec.astype(jnp.float32)
-    lower_half = vec_wide[..., :half_dim]
-    upper_half = vec_wide[..., half_dim:]
-    return jnp.concatenate([lower_half * cos_table - upper_half * sin_table, upper_half * cos_table + lower_half * sin_table], axis=-1).astype(jnp.bfloat16)
+def head_kernel(nx, ny, hid_ref, w_ref, b_ref, pos_ref, vec_ref, kn_ref, vn_ref, q_ref, own_ref, vecs_ref,
+                hbuf, wbuf, vloc, cos_ref, sin_ref, acc, send, recv):
+    nc = ny // CORES
+    x, y = lax.axis_index('x'), lax.axis_index('y')
+    core, chip = lax.rem(y, CORES), lax.div(y, CORES)
+    partner = {'y': chip * CORES + (1 - core)}
+    rows, width = hid_ref.shape
+    n_out = w_ref.shape[1]
+    heads, dim, _ = kn_ref.shape
+    half = dim // 2
+    piece = rows // ny
+    hp, hw = piece // 2, width // 2
+    x_right, x_left = {'x': lax.rem(x + 1, nx)}, {'x': lax.rem(x + nx - 1, nx)}
+
+    def y_of(d, same=True):
+        return lax.rem(chip + d + nc, nc) * CORES + (core if same else 1 - core)
+
+    c_right, c_left = {'y': y_of(1)}, {'y': y_of(-1)}
+    counter = [0]
+
+    def ids(n):
+        counter[0] += n
+        return list(range(counter[0] - n, counter[0]))
+
+    def copy(src, dst, i, dev):
+        return pltpu.make_async_remote_copy(src_ref=src, dst_ref=dst, send_sem=send.at[i], recv_sem=recv.at[i],
+                                            device_id=dev, device_id_type=MESH)
+
+    started = []
+
+    def start(src, dst, i, dev):
+        cp = copy(src, dst, i, dev)
+        cp.start()
+        started.append(cp)
+
+    def arrived(ref, i):
+        copy(ref, ref, i, partner).wait_recv()
+
+    barrier = pltpu.get_barrier_semaphore()
+    peers = [partner, c_right, c_left, x_right, x_left, {'x': lax.rem(x + 2, nx)}]
+    for dev in peers:
+        pl.semaphore_signal(barrier, inc=1, device_id=dev, device_id_type=MESH)
+    pl.semaphore_wait(barrier, len(peers))
+
+    def span(yy, hf):
+        return pl.ds(pl.multiple_of(yy * piece + hf * hp, hp), hp)
+
+    def full(yy):
+        return pl.ds(pl.multiple_of(yy * piece, piece), piece)
+
+    class Ring:
+        def __init__(self, at, right, left):
+            self.at, self.right, self.left = at, right, left
+            self.ra, self.rb, self.lb, self.la, self.fa, self.fb = ids(6)
+
+        def begin(self):
+            at = self.at
+            start(at('own', 0, 'src'), at(2, 0, 'dst'), self.ra, self.right)
+            start(at('own', 1, 'src'), at(0, 1, 'dst'), self.lb, self.left)
+            start(at('own', 1, 'src'), at(2, 1, 'dst'), self.rb, self.right)
+            start(at('own', 0, 'src'), at(0, 0, 'dst'), self.la, self.left)
+
+        def forward(self):
+            at = self.at
+            arrived(at(2, 0, 'here'), self.ra)
+            start(at(2, 0, 'here'), at(1, 0, 'fwd_right'), self.fa, self.right)
+            arrived(at(0, 1, 'here'), self.lb)
+            start(at(0, 1, 'here'), at(1, 1, 'fwd_left'), self.fb, self.left)
+
+        def near(self):
+            arrived(self.at(2, 1, 'here'), self.rb)
+            arrived(self.at(0, 0, 'here'), self.la)
+
+        def far(self):
+            arrived(self.at(1, 0, 'here'), self.fa)
+            arrived(self.at(1, 1, 'here'), self.fb)
+
+    def h_at(slot, hf, role):
+        if slot == 'own':
+            return hid_ref.at[span(y, hf)]
+        return hbuf.at[slot, span(y, hf)]
+
+    def w_at(slot, hf, role):
+        if slot == 'own':
+            return w_ref.at[pl.ds(hf * hw, hw)]
+        return wbuf.at[slot, pl.ds(hf * hw, hw)]
+
+    def x_at(j):
+        def at(slot, hf, role):
+            if slot == 'own' or role == 'dst':
+                return hbuf.at[j, span(y, hf)]
+            shift = {0: 1, 1: 2, 2: -1}[slot]
+            if role == 'fwd_right':
+                shift = -1
+            elif role == 'fwd_left':
+                shift = 1
+            return hbuf.at[j, span(y_of(shift), hf)]
+        return at
+
+    h_ring = Ring(h_at, x_right, x_left)
+    w_ring = Ring(w_at, x_right, x_left)
+    x_rings = [Ring(x_at(j), c_right, c_left) for j in range(3)]
+    d2d = [ids(nc) for _ in range(3)]
+    vec_ids = ids(nx - 1)
+
+    n_vec = vec_ref.shape[0] // width
+    for i in range(n_vec):
+        vloc[i:i + 1, :] = vec_ref[pl.ds(i * width, width)].reshape(1, width).astype(F32)
+    x_cols = pl.ds(pl.multiple_of(x * width, width), width)
+    h_ring.begin()
+    w_ring.begin()
+    for d in range(1, nx):
+        start(vloc, vecs_ref.at[:, x_cols], vec_ids[d - 1], {'x': lax.rem(x + d, nx)})
+
+    freq = jnp.exp(lax.broadcasted_iota(jnp.int32, (half, rows), 0).astype(F32) * (-2.0 * math.log(ROPE_BASE) / dim))
+    angle = pos_ref[...].astype(F32) * freq
+    cos_ref[...] = jnp.cos(angle)
+    sin_ref[...] = jnp.sin(angle)
+
+    def product(w, h):
+        return lax.dot_general(w.T, h, (((1,), (1,)), ((), ())), preferred_element_type=F32)
+
+    acc[...] = product(w_ref[...], hid_ref[...])
+    vecs_ref[:, x_cols] = vloc[...]
+
+    def to_partner(j, d):
+        ref = hbuf.at[j, full(y_of(d))]
+        start(ref, ref, d2d[j][d % nc], partner)
+
+    h_ring.forward()
+    h_ring.near()
+    for j in (2, 0):
+        x_rings[j].begin()
+        to_partner(j, 0)
+    w_ring.forward()
+    h_ring.far()
+    x_rings[1].begin()
+    to_partner(1, 0)
+    for j in (2, 0, 1):
+        x_rings[j].forward()
+        x_rings[j].near()
+        to_partner(j, 1)
+        to_partner(j, -1)
+    w_ring.near()
+    w_ring.far()
+    for j in (2, 0, 1):
+        x_rings[j].far()
+        to_partner(j, 2)
+    for j in (2, 0, 1):
+        for d in range(nc):
+            arrived(hbuf.at[j, full(y_of(d, False))], d2d[j][d])
+        acc[...] += product(wbuf[j], hbuf[j])
+
+    per = own_ref.shape[0]
+    first = pl.multiple_of(x * (rows // nx) + (core * nc + chip) * per, per)
+    own_ref[:, x_cols] = hid_ref[pl.ds(first, per), :]
+    for j in range(3):
+        cols = pl.ds(pl.multiple_of(lax.rem(x + j + 1, nx) * width, width), width)
+        own_ref[:, cols] = hbuf[j, pl.ds(first, per), :]
+
+    bias = jnp.broadcast_to(b_ref[...].reshape(1, n_out).astype(F32), (128, n_out)).T
+
+    def part(h, which, cols):
+        base = (h * 3 + which) * dim
+        v = acc[pl.ds(base, dim), cols]
+        return (v + bias[base:base + dim, 0:1]).astype(BF16)
+
+    def rotate(v, cols):
+        c, s = cos_ref[:, cols], sin_ref[:, cols]
+        lo, up = v[:half].astype(F32), v[half:].astype(F32)
+        return jnp.concatenate([lo * c - up * s, up * c + lo * s], axis=0).astype(BF16)
+
+    own = q_ref.shape[2]
+    own_cols = pl.ds(pl.multiple_of(x * own, own), own)
+    for h in range(heads):
+        q_ref[h] = rotate(part(h, 0, own_cols), own_cols)
+        kn_ref[h] = rotate(part(h, 1, slice(None)), slice(None))
+        vn_ref[h] = part(h, 2, slice(None))
+    for d in range(1, nx):
+        cols = pl.ds(pl.multiple_of(lax.rem(x + nx - d, nx) * width, width), width)
+        arrived(vecs_ref.at[:, cols], vec_ids[d - 1])
+    for cp in started:
+        cp.wait_send()
+
+
+def head(nx, ny, hidden, w_qkv, b_qkv, positions, vecs, heads, dim):
+    rows, width = hidden.shape
+    n_out = w_qkv.shape[1]
+    n_vec = vecs.shape[0] // width
+    vm = pl.BlockSpec(memory_space=pltpu.VMEM)
+    n_sem = 6 * 5 + 3 * (ny // CORES) + nx - 1
+    shape = jax.ShapeDtypeStruct
+    return pl.pallas_call(
+        functools.partial(head_kernel, nx, ny),
+        out_shape=(shape((heads, dim, rows), BF16), shape((heads, dim, rows), BF16),
+                   shape((heads, dim, rows // nx), BF16), shape((rows // (nx * ny), width * nx), BF16),
+                   shape((n_vec, width * nx), F32)),
+        in_specs=[vm] * 5,
+        out_specs=(vm,) * 5,
+        scratch_shapes=[pltpu.VMEM((3, rows, width), BF16), pltpu.VMEM((3, width, n_out), BF16),
+                        pltpu.VMEM((n_vec, width), F32), pltpu.VMEM((dim // 2, rows), F32),
+                        pltpu.VMEM((dim // 2, rows), F32), pltpu.VMEM((n_out, rows), F32),
+                        pltpu.SemaphoreType.DMA((n_sem,)), pltpu.SemaphoreType.DMA((n_sem,))],
+        compiler_params=pltpu.CompilerParams(collective_id=1, has_side_effects=True),
+        name='head',
+    )(hidden, w_qkv, b_qkv, positions.reshape(1, rows), vecs)
 
 
 def solution(mesh):
@@ -250,31 +448,21 @@
     in_specs = (P('dp', 'x'), P('x', 'y'), P('y'), P('y', 'x'), width_spec, width_spec, width_spec, P('x', None, 'y'), P(None, 'y'), P('y', 'x'), width_spec, width_spec, width_spec, cache_spec, cache_spec, P('dp'), P('dp'))
     out_specs = (P('dp', 'x'), cache_spec, cache_spec)
 
+    def shifted(w, d):
+        return lax.ppermute(w, 'x', [((i + d) % nx, i) for i in range(nx)])
+
     def local_step(hidden, w_qkv, b_qkv, w_out, b_out, attn_gain, attn_shift, w_up, b_up, w_down, b_down, mlp_gain, mlp_shift, k_cache, v_cache, positions, lengths):
-        row_count, width_local = hidden.shape
-        local_heads, head_dim = k_cache.shape[2], k_cache.shape[3]
-        x, y = lax.axis_index('x'), lax.axis_index('y')
-        hidden_all = lax.all_gather(hidden, 'x', axis=1, tiled=True)
-        wqkv_all = lax.all_gather(w_qkv, 'x', axis=0, tiled=True)
-        vecs = jnp.stack([b_out, attn_gain, attn_shift, b_down, mlp_gain, mlp_shift, b_out, b_out])
-        vecs = lax.all_gather(vecs, 'x')
-        wo = lax.all_gather(w_out, 'x')
-        wup = lax.all_gather(jnp.transpose(w_up, (1, 0, 2)), 'x')
-        wdn = lax.all_gather(w_down, 'x')
-        qkv_vals = (jnp.dot(hidden_all, wqkv_all, preferred_element_type=jnp.float32) + b_qkv.astype(jnp.float32)).astype(jnp.bfloat16)
-        qkv_vals = qkv_vals.reshape(row_count, local_heads, 3, head_dim)
-        heads_first = lambda v: jnp.transpose(v, (1, 2, 0))
-        per_x = row_count // nx
-        q_t = heads_first(apply_rotary(qkv_vals[:, :, 0], positions))
-        q_own = lax.dynamic_slice_in_dim(q_t, x * per_x, per_x, 2)
-        k_new = heads_first(apply_rotary(qkv_vals[:, :, 1], positions))
-        v_new = heads_first(qkv_vals[:, :, 2])
+        heads, dim = k_cache.shape[2], k_cache.shape[3]
+        vecs = jnp.concatenate([b_out, attn_gain, attn_shift, b_down, mlp_gain, mlp_shift, b_out, b_out])
+        w_up = jnp.transpose(w_up, (1, 0, 2))
+        k_new, v_new, q_own, hid_own, vecs = head(nx, ny, hidden, w_qkv, b_qkv, positions, vecs, heads, dim)
+        q_own, w_out, w_up, w_down = lax.optimization_barrier((q_own, w_out, w_up, w_down))
+        wo = [w_out] + [shifted(w_out, d) for d in range(1, nx)]
+        wup = [w_up] + [shifted(w_up, d) for d in range(1, nx)]
+        wdn = [w_down] + [shifted(w_down, d) for d in range(1, nx)]
         k_t, v_t = jnp.transpose(k_cache, (1, 2, 3, 0)), jnp.transpose(v_cache, (1, 2, 3, 0))
         k_t, v_t, attn_own = cache_step(k_t, v_t, k_new, v_new, q_own, lengths)
         k_full, v_full = jnp.transpose(k_t, (3, 0, 1, 2)), jnp.transpose(v_t, (3, 0, 1, 2))
-        per = per_x // ny
-        blk = lax.rem(y, CORES) * (ny // CORES) + lax.div(y, CORES)
-        hid_own = lax.dynamic_slice_in_dim(hidden_all, x * per_x + blk * per, per, 0)
         result = tail(nx, ny, attn_own, hid_own, wo, vecs, wup, b_up, wdn)
         return result, k_full, v_full
 

time: 153 us -> 163 us (1.065)
  blocking collectives: 37.5 us -> 0 us
  Pallas kernels: 75.6 us -> 105 us
  waiting for transfers between devices: 12.7 us -> 33.2 us
  between operations: 14.1 us -> 0.8 us
  starting transfers between devices: 0.18 us -> 9.93 us
  local copies, waits for them, and re-layouts: 5.93 us -> 12.1 us
  matrix products: 2.61 us -> 0 us
  other arithmetic: 2.84 us -> 0.69 us
    all_gather x3 -> x0, blocking collectives: 37.5 us -> none  [the longest x1 14.4 us: local_step(): wqkv_all = lax.all_gather(w_qkv, 'x', axis=0, tiled=True)]
    ppermute x0 -> x9, waiting for transfers between devices: none -> 33.2 us  [shifted(): return lax.ppermute(w, 'x', [((i + d) % nx, i) for i in range(nx)])]
    pallas_call x0 -> x1, Pallas kernels: none -> 27.4 us  [head(): pl.pallas_call(functools.partial(head_kernel, nx, ny), out_shape=(shape((...]
    all_gather x3 -> x0, waiting for transfers between devices: 11.2 us -> none  [the longest x1 11.2 us: local_step(): wup = lax.all_gather(jnp.transpose(w_up, (1, 0, 2)), 'x')]
    ppermute x0 -> x9, starting transfers between devices: none -> 9.93 us  [shifted(): return lax.ppermute(w, 'x', [((i + d) % nx, i) for i in range(nx)])]
    unnamed x24 -> x31, local copies, waits for them, and re-layouts: 3.81 us -> 10.7 us
    dot_general x1 -> x0, matrix products: 2.61 us -> none  [local_step(): jnp.dot(hidden_all, wqkv_all, preferred_element_type=jnp.float32)]
    pallas_call x1, Pallas kernels: 38.7 us -> 40.7 us  [tail(): pl.pallas_call(functools.partial(tail_kernel, nx, ny), out_shape=jax.Shap...]
  transfers between devices with their start and end apart: 3 -> 9, of which waited for: 1 -> 3; matrix products, arithmetic and copies ran while one was open for 6% -> 1% of each run, Pallas kernels for 24% -> 23%
where the time goes in v3:
time: 163 us; the launch traced here: 162 us
  Pallas kernels  105 us (64%)
  waiting for transfers between devices  33.2 us (20%)
  local copies, waits for them, and re-layouts  12.1 us (7%)
  starting transfers between devices  9.93 us (6%)
    pallas_call x1, Pallas kernels, tail(): pl.pallas_call(functools.partial(tail_kernel, nx, ny), out_shape=jax.Shap...  40.7 us
    pallas_call x1, Pallas kernels, cache_step(): pl.pallas_call(functools.partial(cache_kernel, n), grid=(2 * n,), out_sha...  36.9 us
    ppermute x9, waiting for transfers between devices, shifted(): return lax.ppermute(w, 'x', [((i + d) % nx, i) for i in range(nx)])  33.2 us
    pallas_call x1, Pallas kernels, head(): pl.pallas_call(functools.partial(head_kernel, nx, ny), out_shape=(shape((...  27.4 us
    unnamed x31, local copies, waits for them, and re-layouts  10.7 us
    ppermute x9, starting transfers between devices, shifted(): return lax.ppermute(w, 'x', [((i + d) % nx, i) for i in range(nx)])  9.93 us
  transfers between devices with their start and end apart: 9, of which 3 were waited for; matrix products, arithmetic and copies ran while one was open for 1% of the time, Pallas kernels for 23%

profile of v3, /device:TPU:97, one launch (start us, length us, event | category | flops | bytes accessed | tf_op | source)
XLA Modules:
  0.0 161.7 jit_solution(12689995636401262262)
XLA Ops:
  0.6 1.1 copy.22
  1.7 0.0 copy-start
  1.8 0.9 dynamic-update-slice
  2.6 0.8 dynamic-update-slice.1
  3.5 0.8 dynamic-update-slice.2
  4.3 0.8 dynamic-update-slice.3
  5.1 0.8 dynamic-update-slice.4
  6.0 0.8 dynamic-update-slice.5
  6.8 0.8 dynamic-update-slice.6
  7.6 0.8 dynamic-update-slice.7.vec_ref
  8.5 0.6 copy-done.10
  9.0 27.4 %head.1 = (bf16[2,64,1024]{2,1,0:T(8,128)(2,1)}, bf16[2,64,1024]{2,1,0:T(8,128)(2,1)}, bf16[2,64,256]{2,1,0:T(8,128)(2,1)}, bf16[32,1024]{1,0:T(8,128)(2,1)}, f32[8,1024]{1,0:T(8,128)}) custom-call(bf16[1024,256]{1,0:T(8,128)(2,1)} %hid_ref.1, bf16[256,384]{1,0:T(8,128)(2,1)} %w_ref.1, bf16[384]{0:T(512)(128)(2,1)} %b_ref.1, s32[1,1024]{1,0:T(1,128)} %bitcast.18, ...), custom_call_target="tpu_custom_call" | custom-call | tf_op jit(solution)/shard_map/head/pallas_call | solution.py:428
  36.4 1.7 %collective-permute-start.6 = (bf16[512,256]{1,0:T(8,128)(2,1)}, bf16[512,256]{1,0:T(8,128)(2,1)S(1)}, u32[]{:S(2)}, u32[]{:S(2)}) collective-permute-start(bf16[512,256]{1,0:T(8,128)(2,1)} %refs_8_), channel_id=1, source_target_pairs={{8,0},{16,8},{24,16},{0,24},{9,1},{17,9},{25,17},{1,25},{10,2},{18... | collective-permute-start | bytes 786440 | tf_op jit(solution)/shard_map/ppermute | solution.py:452
  38.2 0.1 collective-permute-start.3
  38.3 1.5 collective-permute-start.4
  39.8 0.0 collective-permute-start.5
  39.8 2.7 %collective-permute-start = (bf16[128,256]{1,0:T(8,128)(2,1)}, bf16[128,256]{1,0:T(8,128)(2,1)S(1)}, u32[]{:S(2)}, u32[]{:S(2)}) collective-permute-start(bf16[128,256]{1,0:T(8,128)(2,1)} %refs_0_), channel_id=1, source_target_pairs={{8,0},{16,8},{24,16},{0,24},{9,1},{17,9},{25,17},{1,25},{10,2},{18... | collective-permute-start | bytes 196616 | tf_op jit(solution)/shard_map/ppermute | solution.py:452
  42.5 26.0 %collective-permute-done.refs_1_ = bf16[128,256]{1,0:T(8,128)(2,1)S(1)} collective-permute-done((bf16[128,256]{1,0:T(8,128)(2,1)}, bf16[128,256]{1,0:T(8,128)(2,1)S(1)}, u32[]{:S(2)}, u32[]{:S(2)}) %collective-permute-start) | collective-permute-done | bytes 65568 | tf_op jit(solution)/shard_map/ppermute | solution.py:452
  68.5 1.5 collective-permute-start.1
  69.9 3.2 %collective-permute-done.1.refs_2_ = bf16[128,256]{1,0:T(8,128)(2,1)S(1)} collective-permute-done((bf16[128,256]{1,0:T(8,128)(2,1)}, bf16[128,256]{1,0:T(8,128)(2,1)S(1)}, u32[]{:S(2)}, u32[]{:S(2)}) %collective-permute-start.1) | collective-permute-done | bytes 65568 | tf_op jit(solution)/shard_map/ppermute | solution.py:452
  73.1 0.4 collective-permute-start.2
  73.5 4.0 %collective-permute-done.2.refs_3_ = bf16[128,256]{1,0:T(8,128)(2,1)S(1)} collective-permute-done((bf16[128,256]{1,0:T(8,128)(2,1)}, bf16[128,256]{1,0:T(8,128)(2,1)S(1)}, u32[]{:S(2)}, u32[]{:S(2)}) %collective-permute-start.2) | collective-permute-done | bytes 65568 | tf_op jit(solution)/shard_map/ppermute | solution.py:452
  77.6 0.9 collective-permute-start.7
  78.4 0.0 collective-permute-done.6.refs_9_
  78.4 1.2 collective-permute-start.8
  79.6 0.7 convert_element_type.3
  80.3 0.6 broadcast_in_dim.2.lane_ref
  80.9 36.9 %cache_step.1 = (bf16[64,2,64,1024]{3,2,1,0:T(8,128)(2,1)}, bf16[64,2,64,1024]{3,2,1,0:T(8,128)(2,1)}, bf16[256,128]{1,0:T(8,128)(2,1)}) custom-call(bf16[64,2,64,1024]{3,2,1,0:T(8,128)(2,1)} %bitcast.10, bf16[64,2,64,1024]{3,2,1,0:T(8,128)(2,1)} %bitcast.11, bf16[2,64,1024]{2,1,0:T(8,128)(2,1)} %get-tuple-element.15.kn_ref, ...), custom_call_target="tpu_custom_call" | custom-call | flops 335544320 | bytes 67108864 | tf_op jit(solution)/shard_map/cache_step/pallas_call | solution.py:223
  117.8 0.0 copy-done
  117.8 0.0 copy-done.7
  117.8 0.0 copy-done.8
  117.9 0.0 copy-done.9
  117.9 0.0 copy-done.4
  117.9 0.0 collective-permute-done.7.refs_10_
  117.9 0.0 copy-start.5
  117.9 0.0 collective-permute-done.8.refs_11_
  117.9 0.0 copy-start.6
  117.9 0.0 collective-permute-done.3.refs_5_
  117.9 0.0 collective-permute-done.4.refs_6_
  118.0 0.0 collective-permute-done.5.refs_7_
  118.0 0.0 copy-start.3
  118.0 0.6 copy-done.5
  118.6 0.1 copy-done.6
  118.7 0.2 copy-done.1
  118.9 0.1 copy-done.2
  119.0 0.2 copy-done.3
  119.2 40.7 %tail.1 = bf16[4,8,32,256]{3,2,1,0:T(8,128)(2,1)} custom-call(bf16[256,128]{1,0:T(8,128)(2,1)} %get-tuple-element.19.attn_ref, bf16[32,1024]{1,0:T(8,128)(2,1)} %get-tuple-element.20.hid_ref, f32[8,1024]{1,0:T(8,128)} %get-tuple-element.21.vec_ref, bf16[2,512]{1,0:T(2,128)(2,1)} %bup_ref.1, bf16[128,256]{1,0:T(8,128)(2,1)} %refs_0_, ...), custom_call_target="tpu_custom_call" | custom-call | tf_op jit(solution)/shard_map/tail/pallas_call | solution.py:142
  159.9 1.9 %copy.32 = bf16[1024,256]{1,0:T(8,128)(2,1)} copy(bf16[1024,256]{1,0:T(8,128)(2,1)} %bitcast.16) | data formatting | bytes 1048576
  (8 shorter events, 0.0 us)
Async XLA Ops:
  1.7 116.1 %copy-start = (bf16[256,2,512]{2,0,1:T(8,128)(2,1)}, bf16[256,2,512]{2,0,1:T(8,128)(2,1)S(1)}, u32[]{:S(2)}) copy-start(bf16[256,2,512]{2,0,1:T(8,128)(2,1)S(1)} %copy.22) | copy-start | bytes 1572868
  8.5 0.6 copy-start.10
  36.4 42.0 %collective-permute-start.6 = (bf16[512,256]{1,0:T(8,128)(2,1)}, bf16[512,256]{1,0:T(8,128)(2,1)S(1)}, u32[]{:S(2)}, u32[]{:S(2)}) collective-permute-start(bf16[512,256]{1,0:T(8,128)(2,1)} %refs_8_), channel_id=1, source_target_pairs={{8,0},{16,8},{24,16},{0,24},{9,1},{17,9},{25,17},{1,25},{10,2},{18... | collective-permute-start | bytes 786440 | tf_op jit(solution)/shard_map/ppermute | solution.py:452
  38.2 79.7 %collective-permute-start.3 = (bf16[2,256,512]{2,1,0:T(8,128)(2,1)S(1)}, bf16[2,256,512]{2,1,0:T(8,128)(2,1)S(1)}, u32[]{:S(2)}, u32[]{:S(2)}) collective-permute-start(bf16[2,256,512]{2,1,0:T(8,128)(2,1)S(1)} %bitcast.12), channel_id=1, source_target_pairs={{8,0},{16,8},{24,16},{0,24},{9,1},{17,9},{25,17},{1,25},{10,2},{18... | collective-permute-start | bytes 1572872 | tf_op jit(solution)/shard_map/ppermute | solution.py:452
  38.3 79.6 %collective-permute-start.4 = (bf16[2,256,512]{2,1,0:T(8,128)(2,1)S(1)}, bf16[2,256,512]{2,1,0:T(8,128)(2,1)S(1)}, u32[]{:S(2)}, u32[]{:S(2)}) collective-permute-start(bf16[2,256,512]{2,1,0:T(8,128)(2,1)S(1)} %bitcast.13), channel_id=1, source_target_pairs={{16,0},{24,8},{0,16},{8,24},{17,1},{25,9},{1,17},{9,25},{18,2},{26... | collective-permute-start | bytes 1572872 | tf_op jit(solution)/shard_map/ppermute | solution.py:452
  39.8 78.2 %collective-permute-start.5 = (bf16[2,256,512]{2,1,0:T(8,128)(2,1)S(1)}, bf16[2,256,512]{2,1,0:T(8,128)(2,1)S(1)}, u32[]{:S(2)}, u32[]{:S(2)}) collective-permute-start(bf16[2,256,512]{2,1,0:T(8,128)(2,1)S(1)} %bitcast.14), channel_id=1, source_target_pairs={{24,0},{0,8},{8,16},{16,24},{25,1},{1,9},{9,17},{17,25},{26,2},{2,... | collective-permute-start | bytes 1572872 | tf_op jit(solution)/shard_map/ppermute | solution.py:452
  39.8 28.7 %collective-permute-start = (bf16[128,256]{1,0:T(8,128)(2,1)}, bf16[128,256]{1,0:T(8,128)(2,1)S(1)}, u32[]{:S(2)}, u32[]{:S(2)}) collective-permute-start(bf16[128,256]{1,0:T(8,128)(2,1)} %refs_0_), channel_id=1, source_target_pairs={{8,0},{16,8},{24,16},{0,24},{9,1},{17,9},{25,17},{1,25},{10,2},{18... | collective-permute-start | bytes 196616 | tf_op jit(solution)/shard_map/ppermute | solution.py:452
  68.5 49.4 %copy-start.7 = (bf16[128,256]{1,0:T(8,128)(2,1)}, bf16[128,256]{1,0:T(8,128)(2,1)S(1)}, u32[]{:S(2)}) copy-start(bf16[128,256]{1,0:T(8,128)(2,1)S(1)} %collective-permute-done.refs_1_) | copy-start | bytes 196612
  68.5 4.6 %collective-permute-start.1 = (bf16[128,256]{1,0:T(8,128)(2,1)}, bf16[128,256]{1,0:T(8,128)(2,1)S(1)}, u32[]{:S(2)}, u32[]{:S(2)}) collective-permute-start(bf16[128,256]{1,0:T(8,128)(2,1)} %refs_0_), channel_id=1, source_target_pairs={{16,0},{24,8},{0,16},{8,24},{17,1},{25,9},{1,17},{9,25},{18,2},{26... | collective-permute-start | bytes 196616 | tf_op jit(solution)/shard_map/ppermute | solution.py:452
  73.1 44.8 %copy-start.8 = (bf16[128,256]{1,0:T(8,128)(2,1)}, bf16[128,256]{1,0:T(8,128)(2,1)S(1)}, u32[]{:S(2)}) copy-start(bf16[128,256]{1,0:T(8,128)(2,1)S(1)} %collective-permute-done.1.refs_2_) | copy-start | bytes 196612
  73.1 4.5 %collective-permute-start.2 = (bf16[128,256]{1,0:T(8,128)(2,1)}, bf16[128,256]{1,0:T(8,128)(2,1)S(1)}, u32[]{:S(2)}, u32[]{:S(2)}) collective-permute-start(bf16[128,256]{1,0:T(8,128)(2,1)} %refs_0_), channel_id=1, source_target_pairs={{24,0},{0,8},{8,16},{16,24},{25,1},{1,9},{9,17},{17,25},{26,2},{2,... | collective-permute-start | bytes 196616 | tf_op jit(solution)/shard_map/ppermute | solution.py:452
  77.6 40.3 %copy-start.9 = (bf16[128,256]{1,0:T(8,128)(2,1)}, bf16[128,256]{1,0:T(8,128)(2,1)S(1)}, u32[]{:S(2)}) copy-start(bf16[128,256]{1,0:T(8,128)(2,1)S(1)} %collective-permute-done.2.refs_3_) | copy-start | bytes 196612
  77.6 40.3 %collective-permute-start.7 = (bf16[512,256]{1,0:T(8,128)(2,1)}, bf16[512,256]{1,0:T(8,128)(2,1)S(1)}, u32[]{:S(2)}, u32[]{:S(2)}) collective-permute-start(bf16[512,256]{1,0:T(8,128)(2,1)} %refs_8_), channel_id=1, source_target_pairs={{16,0},{24,8},{0,16},{8,24},{17,1},{25,9},{1,17},{9,25},{18,2},{26... | collective-permute-start | bytes 786440 | tf_op jit(solution)/shard_map/ppermute | solution.py:452
  78.4 39.4 %copy-start.4 = (bf16[512,256]{1,0:T(8,128)(2,1)}, bf16[512,256]{1,0:T(8,128)(2,1)S(1)}, u32[]{:S(2)}) copy-start(bf16[512,256]{1,0:T(8,128)(2,1)S(1)} %collective-permute-done.6.refs_9_) | copy-start | bytes 786436
  78.4 39.5 %collective-permute-start.8 = (bf16[512,256]{1,0:T(8,128)(2,1)}, bf16[512,256]{1,0:T(8,128)(2,1)S(1)}, u32[]{:S(2)}, u32[]{:S(2)}) collective-permute-start(bf16[512,256]{1,0:T(8,128)(2,1)} %refs_8_), channel_id=1, source_target_pairs={{24,0},{0,8},{8,16},{16,24},{25,1},{1,9},{9,17},{17,25},{26,2},{2,... | collective-permute-start | bytes 786440 | tf_op jit(solution)/shard_map/ppermute | solution.py:452
  117.9 0.7 copy-start.5
  117.9 0.8 copy-start.6
  117.9 1.0 copy-start.1
  118.0 1.1 copy-start.2
  118.0 1.2 copy-start.3

commit v4 on v3

--- a/solution.py
+++ b/solution.py
@@ -12,6 +12,7 @@
 ROPE_BASE = 10000.0
 MESH = pl.DeviceIdType.MESH
 CORES = 2
+N_VEC = 6
 F32 = jnp.float32
 BF16 = jnp.bfloat16
 
@@ -23,9 +24,8 @@
     return (cent * lax.rsqrt(var_row + LN_EPS) * gain + shift).astype(BF16)
 
 
-def tail_kernel(nx, ny, attn_ref, hid_ref, vec_ref, bup_ref, *refs):
-    wo_ref, wup_ref, wdn_ref = refs[:nx], refs[nx:2 * nx], refs[2 * nx:3 * nx]
-    (out_ref, part1, dbuf1, sbuf1, rbuf1, part2, dbuf2, sbuf2, rbuf2, zall, obuf, send, recv) = refs[3 * nx:]
+def tail_kernel(nx, ny, attn_ref, hid_ref, vec_ref, bup_ref, wo_own, wo_all, wup_own, wup_near, wdn_own, out_ref,
+                part1, dbuf1, sbuf1, rbuf1, part2, dbuf2, sbuf2, rbuf2, zall, obuf, wup_far, wdn_buf, send, recv):
     nc = ny // CORES
     x, y = lax.axis_index('x'), lax.axis_index('y')
     core, chip = lax.rem(y, CORES), lax.div(y, CORES)
@@ -60,6 +60,29 @@
 
     def x_cols(d):
         return pl.ds(pl.multiple_of(x_at(d) * width, width), width)
+
+    hd = wdn_own.shape[0] // 2
+    x_right, x_left = {'x': x_at(1)}, {'x': x_at(-1)}
+    first = 2 * nc + 2 * (2 * nc - 1) + nx
+    lo, hi = pl.ds(0, hd), pl.ds(hd, hd)
+    early = [copy(wdn_own.at[lo], wdn_buf.at[2, lo], first, x_right),
+             copy(wdn_own.at[hi], wdn_buf.at[0, hi], first + 1, x_left),
+             copy(wdn_own.at[hi], wdn_buf.at[2, hi], first + 2, x_right),
+             copy(wdn_own.at[lo], wdn_buf.at[0, lo], first + 3, x_left),
+             copy(wup_near.at[1, 0], wup_far.at[0], first + 4, x_right),
+             copy(wup_near.at[0, 1], wup_far.at[1], first + 5, x_left)]
+    for cp in early:
+        cp.start()
+    wo_ref = [wo_own, wo_all.at[0], wo_all.at[1], wo_all.at[2]]
+    wup_ref = [wup_own, wup_near.at[0], wup_far, wup_near.at[1]]
+    wdn_ref = [wdn_own, wdn_buf.at[0], wdn_buf.at[1], wdn_buf.at[2]]
+    late = [copy(wdn_buf.at[2, lo], wdn_buf.at[1, lo], first + 6, x_right),
+            copy(wdn_buf.at[0, hi], wdn_buf.at[1, hi], first + 7, x_left)]
+
+    def pass_on():
+        for i in (0, 1):
+            early[i].wait_recv()
+            late[i].start()
 
     def scatter_sum(part, dbuf, sbuf, rbuf, base):
         cp = copy(part.at[1 - core], dbuf, base, partner)
@@ -75,12 +98,14 @@
             total = total + rbuf[d - 1].astype(F32)
         return total
 
-    def share(buf_at, base):
+    def share(buf_at, base, meanwhile=None):
         far = [copy(buf_at(blk), buf_at(blk), base + d - 1, chip_dev(d)) for d in range(1, nc)]
         for cp in far:
             cp.start()
         near = [copy(buf_at(blk), buf_at(blk), base + nc - 1, partner)]
         near[0].start()
+        if meanwhile is not None:
+            meanwhile()
         for d in range(1, nc):
             b = core * nc + chip_at(-d)
             copy(buf_at(b), buf_at(b), base + d - 1, chip_dev(d)).wait_recv()
@@ -103,7 +128,9 @@
     h_attn = DEEP_ALPHA * hid_ref[...].astype(F32) + total + vec(0)
     z_own = layer_norm(h_attn, vec(1), vec(2))
     zall[blk] = z_own
-    share(lambda b: zall.at[b], base2)
+    share(lambda b: zall.at[b], base2, pass_on)
+    early[4].wait_recv()
+    early[5].wait_recv()
 
     gate = bup_ref[0:1, :].astype(F32)
     val = bup_ref[1:2, :].astype(F32)
@@ -111,6 +138,10 @@
         zb = zall[:, :, x_cols(b)].reshape(ny * rows, width)
         gate = gate + jnp.dot(zb, wup_ref[b][0], preferred_element_type=F32)
         val = val + jnp.dot(zb, wup_ref[b][1], preferred_element_type=F32)
+    for cp in early[2:4] + late:
+        cp.wait_recv()
+    for cp in early + late:
+        cp.wait_send()
     g = (jax.nn.gelu(gate, approximate=True) * val).astype(BF16)
     for b in range(nx):
         res = jnp.dot(g, wdn_ref[b][...], preferred_element_type=F32).astype(BF16)
@@ -131,110 +162,84 @@
         cp.wait_send()
 
 
-def tail(nx, ny, attn, hid, wo, vecs, wup, bup, wdn):
+def tail(nx, ny, attn, hid, vecs, bup, wo, wo_all, wup, wup_near, wdn):
     nc = ny // CORES
     rows, total_width = hid.shape
     width = total_width // nx
-    n_sem = 2 * nc + 2 * (2 * nc - 1) + nx + 1
+    n_sem = 2 * nc + 2 * (2 * nc - 1) + nx + 8
     vm = pl.BlockSpec(memory_space=pltpu.VMEM)
     reduce_bufs = [pltpu.VMEM((CORES, nc, rows, total_width), BF16), pltpu.VMEM((nc, rows, total_width), BF16),
                    pltpu.VMEM((nc, rows, total_width), BF16), pltpu.VMEM((nc - 1, rows, total_width), BF16)]
     out = pl.pallas_call(
         functools.partial(tail_kernel, nx, ny),
         out_shape=jax.ShapeDtypeStruct((nx, ny, rows, width), BF16),
-        in_specs=[vm] * (4 + 3 * nx),
+        in_specs=[vm] * 9,
         out_specs=vm,
         scratch_shapes=reduce_bufs + reduce_bufs + [
             pltpu.VMEM((ny, rows, total_width), BF16), pltpu.VMEM((nx, rows, width), BF16),
+            pltpu.VMEM(wup.shape, BF16), pltpu.VMEM((3,) + wdn.shape, BF16),
             pltpu.SemaphoreType.DMA((n_sem,)), pltpu.SemaphoreType.DMA((n_sem,))],
-        compiler_params=pltpu.CompilerParams(collective_id=0, has_side_effects=True),
+        compiler_params=pltpu.CompilerParams(collective_id=0, has_side_effects=True, vmem_limit_bytes=16 * 2**20),
         name='tail',
-    )(attn, hid, vecs, bup, *wo, *wup, *wdn)
+    )(attn, hid, vecs, bup, wo, wo_all, wup, wup_near, wdn)
     return out.reshape(nx * ny * rows, width)
 
 
-def cache_kernel(n_blocks, k_ref, v_ref, kn_ref, vn_ref, q_ref, lens_ref, lane_ref, ko_ref, vo_ref, attn_ref,
-                 qs, sc, acc):
-    step = pl.program_id(0)
-    slots, heads, dim, _ = k_ref.shape
+def update_and_attend(k_ref, v_ref, kn_ref, vn_ref, q_ref, lens_ref, attn_ref, lane, qs, sc, acc, slots, k_here, v_here):
+    total_slots, heads, dim, rows = k_ref.shape
+    n = total_slots // slots
     own = q_ref.shape[2]
     cols = pl.ds(pl.multiple_of(lax.axis_index('x') * own, own), own)
-    total_slots = n_blocks * slots
-
-    @pl.when(step == 0)
-    def _():
-        qs[...] = q_ref[...].astype(F32)
-        acc[...] = jnp.zeros_like(acc)
-
-    def write(src, new, dst, first):
+    lane[...] = jnp.broadcast_to(lens_ref[...].astype(F32), lane.shape).astype(BF16)
+    qs[...] = q_ref[...].astype(F32)
+    acc[...] = jnp.zeros_like(acc)
+
+    def write(ref, new, first):
         for s in range(slots):
-            hit = lane_ref[...] == (first + s).astype(F32).astype(BF16)
+            hit = lane[...] == (first + s).astype(F32).astype(BF16)
             for h in range(heads):
                 for t in range(dim // 16):
                     part = pl.ds(t * 16, 16)
-                    dst[s, h, part, :] = jnp.where(hit, new[h, part, :], src[s, h, part, :])
-
-    @pl.when(step < n_blocks)
-    def _():
-        first = step * slots
-        write(k_ref, kn_ref, ko_ref, first)
+                    ref[first + s, h, part, :] = jnp.where(hit, new[h, part, :], ref[first + s, h, part, :])
+
+    def k_step(i, carry):
+        first = i * slots
+        write(k_ref, kn_ref, first)
         for s in range(slots):
             for h in range(heads):
                 sc[h, pl.ds(first + s, 1), :] = jnp.sum(
-                    ko_ref[s, h, :, cols].astype(F32) * qs[h], axis=0, keepdims=True)
-
-    @pl.when(step == n_blocks - 1)
-    def _():
-        slot = lax.broadcasted_iota(jnp.int32, (total_slots, own), 0)
-        ok = slot <= lens_ref[:, cols]
-        for h in range(heads):
-            s = jnp.where(ok, sc[h] * (dim ** -0.5), -1e30)
-            e = jnp.exp(s - jnp.max(s, axis=0, keepdims=True))
-            p = e / jnp.sum(e, axis=0, keepdims=True)
-            sc[h] = p.astype(BF16).astype(F32)
-
-    @pl.when(step >= n_blocks)
-    def _():
-        first = (step - n_blocks) * slots
-        write(v_ref, vn_ref, vo_ref, first)
+                    k_ref[first + s, h, :, cols].astype(F32) * qs[h], axis=0, keepdims=True)
+        return carry
+
+    k_here()
+    lax.fori_loop(0, n, k_step, 0)
+    slot_id = lax.broadcasted_iota(jnp.int32, (total_slots, own), 0)
+    ok = slot_id <= lens_ref[:, cols]
+    for h in range(heads):
+        s = jnp.where(ok, sc[h] * (dim ** -0.5), -1e30)
+        e = jnp.exp(s - jnp.max(s, axis=0, keepdims=True))
+        p = e / jnp.sum(e, axis=0, keepdims=True)
+        sc[h] = p.astype(BF16).astype(F32)
+
+    def v_step(i, carry):
+        first = i * slots
+        write(v_ref, vn_ref, first)
         for h in range(heads):
             a = acc[h]
             for s in range(slots):
-                a = a + vo_ref[s, h, :, cols].astype(F32) * sc[h, pl.ds(first + s, 1), :]
+                a = a + v_ref[first + s, h, :, cols].astype(F32) * sc[h, pl.ds(first + s, 1), :]
             acc[h] = a
-
-    @pl.when(step == 2 * n_blocks - 1)
-    def _():
-        attn_ref[...] = acc[...].reshape(heads * dim, own).T.astype(BF16)
-
-
-def cache_step(k_t, v_t, k_new, v_new, q_own, lengths, slots=4):
-    total_slots, heads, dim, rows = k_t.shape
-    own = q_own.shape[2]
-    n = total_slots // slots
-    blk = (slots, heads, dim, rows)
-    lens = lengths.reshape(1, rows)
-    lane = jnp.broadcast_to(lengths.astype(BF16)[None], (16, rows))
-    k_spec = pl.BlockSpec(blk, lambda i: (jnp.minimum(i, n - 1), 0, 0, 0))
-    v_spec = pl.BlockSpec(blk, lambda i: (jnp.maximum(i - n, 0), 0, 0, 0))
-    whole = pl.BlockSpec(memory_space=pltpu.VMEM)
-    shape = jax.ShapeDtypeStruct(k_t.shape, k_t.dtype)
-    size = 4 * k_t.size * 2
-    return pl.pallas_call(
-        functools.partial(cache_kernel, n),
-        grid=(2 * n,),
-        out_shape=(shape, shape, jax.ShapeDtypeStruct((own, heads * dim), BF16)),
-        in_specs=[k_spec, v_spec] + [whole] * 5,
-        out_specs=(k_spec, v_spec, whole),
-        scratch_shapes=[pltpu.VMEM((heads, dim, own), F32), pltpu.VMEM((heads, total_slots, own), F32),
-                        pltpu.VMEM((heads, dim, own), F32)],
-        cost_estimate=pl.CostEstimate(flops=40 * k_t.size, bytes_accessed=size, transcendentals=0),
-        name='cache_step',
-    )(k_t, v_t, k_new, v_new, q_own, lens, lane)
-
-
-def head_kernel(nx, ny, hid_ref, w_ref, b_ref, pos_ref, vec_ref, kn_ref, vn_ref, q_ref, own_ref, vecs_ref,
-                hbuf, wbuf, vloc, cos_ref, sin_ref, acc, send, recv):
+        return carry
+
+    v_here()
+    lax.fori_loop(0, n, v_step, 0)
+    attn_ref[...] = acc[...].reshape(heads * dim, own).T.astype(BF16)
+
+
+def head_kernel(nx, ny, hid_ref, w_ref, b_ref, pos_ref, lens_ref, wo_ref, wup_ref, k_ref, v_ref, *refs):
+    vec_refs, (attn_ref, own_ref, vecs_ref, wo_all, wup_near, kc_ref, vc_ref, kn_ref, vn_ref, q_ref,
+               lane, qs, sc, att,
+               hbuf, wbuf, vloc, cos_ref, sin_ref, acc, send, recv, load) = refs[:N_VEC], refs[N_VEC:]
     nc = ny // CORES
     x, y = lax.axis_index('x'), lax.axis_index('y')
     core, chip = lax.rem(y, CORES), lax.div(y, CORES)
@@ -273,6 +278,12 @@
 
     barrier = pltpu.get_barrier_semaphore()
     peers = [partner, c_right, c_left, x_right, x_left, {'x': lax.rem(x + 2, nx)}]
+    n_load = load.shape[1]
+    step = k_ref.shape[0] // n_load
+    loads = [pltpu.make_async_copy(src.at[pl.ds(i * step, step)], dst.at[pl.ds(i * step, step)], load.at[j, i])
+             for j, (src, dst) in enumerate(((k_ref, kc_ref), (v_ref, vc_ref))) for i in range(n_load)]
+    for cp in loads:
+        cp.start()
     for dev in peers:
         pl.semaphore_signal(barrier, inc=1, device_id=dev, device_id_type=MESH)
     pl.semaphore_wait(barrier, len(peers))
@@ -332,15 +343,23 @@
             return hbuf.at[j, span(y_of(shift), hf)]
         return at
 
+    ho = wo_ref.shape[0] // 2
+
+    def o_at(slot, hf, role):
+        if slot == 'own':
+            return wo_ref.at[pl.ds(hf * ho, ho)]
+        return wo_all.at[slot, pl.ds(hf * ho, ho)]
+
     h_ring = Ring(h_at, x_right, x_left)
     w_ring = Ring(w_at, x_right, x_left)
+    o_ring = Ring(o_at, x_right, x_left)
+    up_ids = ids(2)
     x_rings = [Ring(x_at(j), c_right, c_left) for j in range(3)]
     d2d = [ids(nc) for _ in range(3)]
     vec_ids = ids(nx - 1)
 
-    n_vec = vec_ref.shape[0] // width
-    for i in range(n_vec):
-        vloc[i:i + 1, :] = vec_ref[pl.ds(i * width, width)].reshape(1, width).astype(F32)
+    for i in range(N_VEC):
+        vloc[i:i + 1, :] = vec_refs[i][...].reshape(1, width).astype(F32)
     x_cols = pl.ds(pl.multiple_of(x * width, width), width)
     h_ring.begin()
     w_ring.begin()
@@ -376,8 +395,13 @@
         x_rings[j].near()
         to_partner(j, 1)
         to_partner(j, -1)
-    w_ring.near()
+        if j == 2:
+            w_ring.near()
+            o_ring.begin()
+            start(wup_ref, wup_near.at[1], up_ids[0], x_right)
+            start(wup_ref, wup_near.at[0], up_ids[1], x_left)
     w_ring.far()
+    o_ring.forward()
     for j in (2, 0, 1):
         x_rings[j].far()
         to_partner(j, 2)
@@ -414,31 +438,52 @@
     for d in range(1, nx):
         cols = pl.ds(pl.multiple_of(lax.rem(x + nx - d, nx) * width, width), width)
         arrived(vecs_ref.at[:, cols], vec_ids[d - 1])
+    o_ring.near()
+
+    def k_here():
+        for cp in loads[:n_load]:
+            cp.wait()
+
+    def v_here():
+        for cp in loads[n_load:]:
+            cp.wait()
+
+    update_and_attend(kc_ref, vc_ref, kn_ref, vn_ref, q_ref, lens_ref, attn_ref, lane, qs, sc, att, 4, k_here, v_here)
+    o_ring.far()
+    arrived(wup_near.at[1], up_ids[0])
+    arrived(wup_near.at[0], up_ids[1])
     for cp in started:
         cp.wait_send()
 
 
-def head(nx, ny, hidden, w_qkv, b_qkv, positions, vecs, heads, dim):
+def head(nx, ny, hidden, w_qkv, b_qkv, positions, lengths, w_out, w_up, k_t, v_t, vecs):
     rows, width = hidden.shape
     n_out = w_qkv.shape[1]
-    n_vec = vecs.shape[0] // width
+    _, heads, dim, _ = k_t.shape
+    n_vec = 8
+    own = rows // nx
     vm = pl.BlockSpec(memory_space=pltpu.VMEM)
-    n_sem = 6 * 5 + 3 * (ny // CORES) + nx - 1
-    shape = jax.ShapeDtypeStruct
+    hbm = pl.BlockSpec(memory_space=pl.ANY)
+    n_sem = 6 * 6 + 2 + 3 * (ny // CORES) + nx - 1
+    shape = pltpu.VMEM
     return pl.pallas_call(
         functools.partial(head_kernel, nx, ny),
-        out_shape=(shape((heads, dim, rows), BF16), shape((heads, dim, rows), BF16),
-                   shape((heads, dim, rows // nx), BF16), shape((rows // (nx * ny), width * nx), BF16),
-                   shape((n_vec, width * nx), F32)),
-        in_specs=[vm] * 5,
-        out_specs=(vm,) * 5,
-        scratch_shapes=[pltpu.VMEM((3, rows, width), BF16), pltpu.VMEM((3, width, n_out), BF16),
+        out_shape=(shape((rows // nx, heads * dim), BF16), shape((rows // (nx * ny), width * nx), BF16),
+                   shape((n_vec, width * nx), F32), shape((3,) + w_out.shape, BF16), shape((2,) + w_up.shape, BF16),
+                   shape(k_t.shape, BF16), shape(v_t.shape, BF16)),
+        in_specs=[vm] * 6 + [hbm] * 3 + [vm] * N_VEC,
+        out_specs=(vm,) * 7,
+        scratch_shapes=[pltpu.VMEM((heads, dim, rows), BF16), pltpu.VMEM((heads, dim, rows), BF16),
+                        pltpu.VMEM((heads, dim, own), BF16), pltpu.VMEM((16, rows), BF16),
+                        pltpu.VMEM((heads, dim, own), F32), pltpu.VMEM((heads, k_t.shape[0], own), F32),
+                        pltpu.VMEM((heads, dim, own), F32), pltpu.VMEM((3, rows, width), BF16), pltpu.VMEM((3, width, n_out), BF16),
                         pltpu.VMEM((n_vec, width), F32), pltpu.VMEM((dim // 2, rows), F32),
                         pltpu.VMEM((dim // 2, rows), F32), pltpu.VMEM((n_out, rows), F32),
-                        pltpu.SemaphoreType.DMA((n_sem,)), pltpu.SemaphoreType.DMA((n_sem,))],
-        compiler_params=pltpu.CompilerParams(collective_id=1, has_side_effects=True),
+                        pltpu.SemaphoreType.DMA((n_sem,)), pltpu.SemaphoreType.DMA((n_sem,)),
+                        pltpu.SemaphoreType.DMA((2, 8))],
+        compiler_params=pltpu.CompilerParams(collective_id=1, has_side_effects=True, vmem_limit_bytes=16 * 2**20),
         name='head',
-    )(hidden, w_qkv, b_qkv, positions.reshape(1, rows), vecs)
+    )(hidden, w_qkv, b_qkv, positions.reshape(1, rows), lengths.reshape(1, rows), w_out, w_up, k_t, v_t, *vecs)
 
 
 def solution(mesh):
@@ -448,22 +493,14 @@
     in_specs = (P('dp', 'x'), P('x', 'y'), P('y'), P('y', 'x'), width_spec, width_spec, width_spec, P('x', None, 'y'), P(None, 'y'), P('y', 'x'), width_spec, width_spec, width_spec, cache_spec, cache_spec, P('dp'), P('dp'))
     out_specs = (P('dp', 'x'), cache_spec, cache_spec)
 
-    def shifted(w, d):
-        return lax.ppermute(w, 'x', [((i + d) % nx, i) for i in range(nx)])
-
     def local_step(hidden, w_qkv, b_qkv, w_out, b_out, attn_gain, attn_shift, w_up, b_up, w_down, b_down, mlp_gain, mlp_shift, k_cache, v_cache, positions, lengths):
-        heads, dim = k_cache.shape[2], k_cache.shape[3]
-        vecs = jnp.concatenate([b_out, attn_gain, attn_shift, b_down, mlp_gain, mlp_shift, b_out, b_out])
+        k_t, v_t = jnp.transpose(k_cache, (1, 2, 3, 0)), jnp.transpose(v_cache, (1, 2, 3, 0))
         w_up = jnp.transpose(w_up, (1, 0, 2))
-        k_new, v_new, q_own, hid_own, vecs = head(nx, ny, hidden, w_qkv, b_qkv, positions, vecs, heads, dim)
-        q_own, w_out, w_up, w_down = lax.optimization_barrier((q_own, w_out, w_up, w_down))
-        wo = [w_out] + [shifted(w_out, d) for d in range(1, nx)]
-        wup = [w_up] + [shifted(w_up, d) for d in range(1, nx)]
-        wdn = [w_down] + [shifted(w_down, d) for d in range(1, nx)]
-        k_t, v_t = jnp.transpose(k_cache, (1, 2, 3, 0)), jnp.transpose(v_cache, (1, 2, 3, 0))
-        k_t, v_t, attn_own = cache_step(k_t, v_t, k_new, v_new, q_own, lengths)
+        vecs = (b_out, attn_gain, attn_shift, b_down, mlp_gain, mlp_shift)
+        attn_own, hid_own, vecs, wo_all, wup_near, k_t, v_t = head(
+            nx, ny, hidden, w_qkv, b_qkv, positions, lengths, w_out, w_up, k_t, v_t, vecs)
+        result = tail(nx, ny, attn_own, hid_own, vecs, b_up, w_out, wo_all, w_up, wup_near, w_down)
         k_full, v_full = jnp.transpose(k_t, (3, 0, 1, 2)), jnp.transpose(v_t, (3, 0, 1, 2))
-        result = tail(nx, ny, attn_own, hid_own, wo, vecs, wup, b_up, wdn)
         return result, k_full, v_full
 
     return jax.shard_map(local_step, mesh=mesh, in_specs=in_specs, out_specs=out_specs, check_vma=False)

time: 163 us -> 93 us (0.57)
  Pallas kernels: 105 us -> 68.9 us
  waiting for transfers between devices: 33.2 us -> 0 us
  local copies, waits for them, and re-layouts: 12.1 us -> 23 us
  starting transfers between devices: 9.93 us -> 0 us
    pallas_call x1 -> x0, Pallas kernels: 36.9 us -> none  [cache_step(): pl.pallas_call(functools.partial(cache_kernel, n), grid=(2 * n,), out_sha...]
    ppermute x9 -> x0, waiting for transfers between devices: 33.2 us -> none  [shifted(): return lax.ppermute(w, 'x', [((i + d) % nx, i) for i in range(nx)])]
    unnamed x31 -> x34, local copies, waits for them, and re-layouts: 10.7 us -> 23 us
    ppermute x9 -> x0, starting transfers between devices: 9.93 us -> none  [shifted(): return lax.ppermute(w, 'x', [((i + d) % nx, i) for i in range(nx)])]
    pallas_call x1, Pallas kernels: 27.4 us -> 31.8 us  [head(): pl.pallas_call(functools.partial(head_kernel, nx, ny), out_shape=(shape((...]
    pallas_call x1, Pallas kernels: 40.7 us -> 37.1 us  [tail(): pl.pallas_call(functools.partial(tail_kernel, nx, ny), out_shape=jax.Shap...]
  transfers between devices with their start and end apart: 9 -> 0, of which waited for: 3 -> 0; matrix products, arithmetic and copies ran while one was open for 1% -> 0% of each run, Pallas kernels for 23% -> 0%
where the time goes in v4:
time: 93 us; the launch traced here: 92.6 us
  Pallas kernels  68.9 us (74%)
  local copies, waits for them, and re-layouts  23 us (25%)
    pallas_call x1, Pallas kernels, tail(): pl.pallas_call(functools.partial(tail_kernel, nx, ny), out_shape=jax.Shap...  37.1 us
    pallas_call x1, Pallas kernels, head(): pl.pallas_call(functools.partial(head_kernel, nx, ny), out_shape=(shape((...  31.8 us
    unnamed x34, local copies, waits for them, and re-layouts  23 us

profile of v4, /device:TPU:97, one launch (start us, length us, event | category | flops | bytes accessed | tf_op | source)
XLA Modules:
  0.0 92.6 jit_solution(8917224397923111290)
XLA Ops:
  0.6 1.1 %copy.22 = bf16[256,2,512]{2,0,1:T(8,128)(2,1)S(1)} copy(bf16[256,2,512]{2,1,0:T(2,128)(2,1)} %param.24) | data formatting | bytes 1048576 | tf_op args[7]
  1.7 0.0 copy-start
  1.7 1.0 %copy-done = bf16[1024,256]{1,0:T(8,128)(2,1)S(1)} copy-done((bf16[1024,256]{1,0:T(8,128)(2,1)S(1)}, bf16[1024,256]{1,0:T(8,128)(2,1)}, u32[]{:S(2)}) %copy-start) | copy-done | bytes 524312
  2.8 0.0 copy-start.1
  2.8 0.8 copy-done.1
  3.6 0.0 copy-start.4
  3.6 0.9 copy-done.4
  4.5 0.0 copy-start.5
  4.5 0.7 copy-done.5
  5.2 0.0 copy-start.6
  5.2 0.7 copy-done.6
  5.9 0.0 copy-start.8
  5.9 0.7 copy-done.8
  6.6 0.0 copy-start.9
  6.6 0.7 copy-done.9
  7.3 0.0 copy-start.10
  7.3 0.7 copy-done.10
  7.9 0.0 copy-start.11
  7.9 0.7 copy-done.11
  8.6 0.0 copy-start.12
  8.6 0.7 copy-done.12
  9.2 0.0 copy-start.13
  9.2 0.7 copy-done.13
  9.9 0.0 copy-start.14
  9.9 0.7 copy-done.14
  10.5 0.0 copy-start.2
  10.5 0.0 copy-start.3
  10.5 0.0 copy-start.7
  10.5 31.8 %head.1 = (bf16[256,128]{1,0:T(8,128)(2,1)S(1)}, bf16[32,1024]{1,0:T(8,128)(2,1)S(1)}, f32[8,1024]{1,0:T(8,128)S(1)}, bf16[3,128,256]{2,1,0:T(8,128)(2,1)S(1)}, ...) custom-call(bf16[1024,256]{1,0:T(8,128)(2,1)S(1)} %copy-done, ...), custom_call_target="tpu_custom_call" | custom-call | tf_op jit(solution)/shard_map/head/pallas_call | solution.py:469
  42.3 0.0 copy-done.2
  42.3 0.0 copy-done.3
  42.3 0.0 copy-done.7
  42.4 37.1 %tail.1 = bf16[4,8,32,256]{3,2,1,0:T(8,128)(2,1)S(1)} custom-call(bf16[256,128]{1,0:T(8,128)(2,1)S(1)} %get-tuple-element.10.attn_ref, bf16[32,1024]{1,0:T(8,128)(2,1)S(1)} %get-tuple-element.11.hid_ref, f32[8,1024]{1,0:T(8,128)S(1)} %get-tuple-element.12.vec_ref, bf16[2,512]{1,0:T(2,128)(2,1)S(1)} %copy-done.7, bf16[128,256]{1,0:T(8,128)(2,1)S(1)} %copy-done.2, ...), custom_call_target="tpu_custom_call" | custom-call | tf_op jit(solution)/shard_map/tail/pallas_call | solution.py:173
  79.5 6.2 %copy.26 = bf16[1024,64,2,64]{0,3,2,1:T(8,128)(2,1)} copy(bf16[1024,64,2,64]{0,3,2,1:T(8,128)(2,1)S(1)} %bitcast.11) | data formatting | bytes 33554432
  85.7 6.2 %copy.27 = bf16[1024,64,2,64]{0,3,2,1:T(8,128)(2,1)} copy(bf16[1024,64,2,64]{0,3,2,1:T(8,128)(2,1)S(1)} %bitcast.10) | data formatting | bytes 33554432
  91.8 0.8 copy.28
Async XLA Ops:
  1.7 1.0 %copy-start = (bf16[1024,256]{1,0:T(8,128)(2,1)S(1)}, bf16[1024,256]{1,0:T(8,128)(2,1)}, u32[]{:S(2)}) copy-start(bf16[1024,256]{1,0:T(8,128)(2,1)} %hid_ref.1) | copy-start | bytes 1572868
  2.8 0.8 copy-start.1
  3.6 0.9 %copy-start.4 = (bf16[256,384]{1,0:T(8,128)(2,1)S(1)}, bf16[256,384]{1,0:T(8,128)(2,1)}, u32[]{:S(2)}) copy-start(bf16[256,384]{1,0:T(8,128)(2,1)} %w_ref.1) | copy-start | bytes 589828
  4.5 0.7 copy-start.5
  5.2 0.7 copy-start.6
  5.9 0.7 copy-start.8
  6.6 0.7 copy-start.9
  7.3 0.7 copy-start.10
  7.9 0.7 copy-start.11
  8.6 0.7 copy-start.12
  9.2 0.7 copy-start.13
  9.9 0.7 copy-start.14
  10.5 31.8 %copy-start.2 = (bf16[128,256]{1,0:T(8,128)(2,1)S(1)}, bf16[128,256]{1,0:T(8,128)(2,1)}, u32[]{:S(2)}) copy-start(bf16[128,256]{1,0:T(8,128)(2,1)} %wo_own.1) | copy-start | bytes 196612
  10.5 31.8 %copy-start.3 = (bf16[512,256]{1,0:T(8,128)(2,1)S(1)}, bf16[512,256]{1,0:T(8,128)(2,1)}, u32[]{:S(2)}) copy-start(bf16[512,256]{1,0:T(8,128)(2,1)} %wdn_own.1) | copy-start | bytes 786436
  10.5 31.8 %copy-start.7 = (bf16[2,512]{1,0:T(2,128)(2,1)S(1)}, bf16[2,512]{1,0:T(2,128)(2,1)}, u32[]{:S(2)}) copy-start(bf16[2,512]{1,0:T(2,128)(2,1)} %bup_ref.1) | copy-start | bytes 6148

commit v5 on v0

v5 whole, which is shorter than its diff:
```python
import functools
import math
import jax
import jax.numpy as jnp
from jax import lax
from jax.experimental import pallas as pl
from jax.experimental.pallas import tpu as pltpu
from jax.sharding import PartitionSpec as P

DEEP_ALPHA = math.sqrt(140.0)
LN_EPS = 1e-5
ROPE_BASE = 10000.0
MESH = pl.DeviceIdType.MESH
CORES = 2
N_VEC = 6
N_LOAD = 1
GROUP = 4
F32 = jnp.float32
BF16 = jnp.bfloat16


def layer_norm(h_val, gain, shift):
    mean_row = jnp.mean(h_val, axis=-1, keepdims=True)
    cent = h_val - mean_row
    var_row = jnp.mean(cent * cent, axis=-1, keepdims=True)
    return (cent * lax.rsqrt(var_row + LN_EPS) * gain + shift).astype(BF16)


def layer_kernel(nx, ny, hid_in, wqkv_in, wo_in, wup_in, wdn_in, bup_in, bqkv_in, pos_in, lens_in, k_in, v_in, *refs):
    vec_in, refs = refs[:N_VEC], refs[N_VEC:]
    out_ref, kc, vc = refs[:3]
    vec_own, refs = refs[3:3 + N_VEC], refs[3 + N_VEC:]
    (hid, wqkv, wo_own, wup_own, wdn_own, bup, bqkv, pos, lens, qpart, qrecv, qown, kvn, qs, sc, lane,
     wo_far, wup_far, wdn_far, vloc, vecs, hid_own, part1, dbuf1, sbuf1, rbuf1, part2, dbuf2, sbuf2, rbuf2,
     zall, obuf, send, recv, load, cache_load) = refs
    nc = ny // CORES
    x, y = lax.axis_index('x'), lax.axis_index('y')
    core, chip = lax.rem(y, CORES), lax.div(y, CORES)
    partner = {'y': chip * CORES + (1 - core)}
    blk = core * nc + chip
    total_slots, heads, dim, all_rows = k_in.shape
    half = dim // 2
    width = hid_in.shape[1]
    own = all_rows // nx
    per = own // ny
    n_out = wqkv_in.shape[1]

    def chip_at(d):
        return lax.rem(chip + d + nc, nc)

    def x_at(d):
        return lax.rem(x + d + nx, nx)

    def chip_dev(d):
        return {'y': chip_at(d) * CORES + core}

    def x_dev(d):
        return {'x': x_at(d)}

    def x_cols(d):
        return pl.ds(pl.multiple_of(x_at(d) * width, width), width)

    def x_rows(d):
        return pl.ds(pl.multiple_of(x_at(d) * own, own), own)

    cols = x_rows(0)
    counter = [0]
    started = []

    def ids(n):
        counter[0] += n
        return list(range(counter[0] - n, counter[0]))

    def copy(src, dst, i, dev):
        return pltpu.make_async_remote_copy(src_ref=src, dst_ref=dst, send_sem=send.at[i], recv_sem=recv.at[i],
                                            device_id=dev, device_id_type=MESH)

    def start(src, dst, i, dev):
        cp = copy(src, dst, i, dev)
        cp.start()
        started.append(cp)

    def arrived(ref, i):
        copy(ref, ref, i, partner).wait_recv()

    pairs = [(hid_in, hid), (wqkv_in, wqkv), (bqkv_in, bqkv), (pos_in, pos), (lens_in, lens), (bup_in, bup),
             (wo_in, wo_own), (wup_in, wup_own), (wdn_in, wdn_own)] + list(zip(vec_in, vec_own))
    loads = [pltpu.make_async_copy(src, dst, load.at[i]) for i, (src, dst) in enumerate(pairs)]
    for cp in loads:
        cp.start()
    step = total_slots // N_LOAD
    cache_loads = [[pltpu.make_async_copy(src.at[pl.ds(i * step, step)], dst.at[pl.ds(i * step, step)],
                                          cache_load.at[j, i]) for i in range(N_LOAD)]
                   for j, (src, dst) in enumerate(((k_in, kc), (v_in, vc)))]

    barrier = pltpu.get_barrier_semaphore()
    peers = [partner] + [chip_dev(d) for d in range(1, nc)] + [x_dev(d) for d in range(1, nx)]
    for dev in peers:
        pl.semaphore_signal(barrier, inc=1, device_id=dev, device_id_type=MESH)
    for cp in loads:
        cp.wait()
    w_t = wqkv[...].T

    def product(d):
        return lax.dot_general(w_t, hid[x_rows(d), :], (((1,), (1,)), ((), ())), preferred_element_type=F32)

    order = [2, 1, 3]
    for d in order:
        qpart[d - 1] = product(d).astype(BF16)
    pl.semaphore_wait(barrier, len(peers))

    q_ids, wo_ids, hid_ids, vec_ids, kv_ids = (ids(nx - 1) for _ in range(5))
    for d in order:
        start(qpart.at[d - 1], qrecv.at[d - 1], q_ids[d - 1], x_dev(d))
    for i in range(N_VEC):
        vloc[i:i + 1, :] = vec_own[i][...].reshape(1, width).astype(F32)

    def my_rows(d):
        return pl.ds(pl.multiple_of(x_at(d) * own + blk * per, per), per)

    for d in order:
        start(wo_own, wo_far.at[d - 1], wo_ids[d - 1], x_dev(d))
        start(hid.at[my_rows(d)], hid_own.at[:, x_cols(0)], hid_ids[d - 1], x_dev(d))
        start(vloc, vecs.at[:, x_cols(0)], vec_ids[d - 1], x_dev(d))

    class Ring:
        def __init__(self, piece, buf):
            self.piece, self.buf = piece, buf
            self.ra, self.rb, self.lb, self.la, self.fa, self.fb = ids(6)

        def begin(self):
            start(self.piece(0), self.buf(2, 0), self.ra, x_dev(1))
            start(self.piece(1), self.buf(0, 1), self.lb, x_dev(-1))
            start(self.piece(1), self.buf(2, 1), self.rb, x_dev(1))
            start(self.piece(0), self.buf(0, 0), self.la, x_dev(-1))

        def forward(self):
            arrived(self.buf(2, 0), self.ra)
            start(self.buf(2, 0), self.buf(1, 0), self.fa, x_dev(1))
            arrived(self.buf(0, 1), self.lb)
            start(self.buf(0, 1), self.buf(1, 1), self.fb, x_dev(-1))

        def near(self):
            arrived(self.buf(2, 1), self.rb)
            arrived(self.buf(0, 0), self.la)

        def far(self):
            arrived(self.buf(1, 0), self.fa)
            arrived(self.buf(1, 1), self.fb)

    hd = wdn_own.shape[0] // 2
    up_ring = Ring(lambda h: wup_own.at[h], lambda s, h: wup_far.at[s, h])
    down_ring = Ring(lambda h: wdn_own.at[pl.ds(h * hd, hd)], lambda s, h: wdn_far.at[s, pl.ds(h * hd, hd)])
    up_ring.begin()
    down_ring.begin()
    for group in cache_loads:
        for cp in group:
            cp.start()

    qown[...] = product(0)
    vecs[:, x_cols(0)] = vloc[...]
    hid_own[:, x_cols(0)] = hid[my_rows(0), :]
    freq = jnp.exp(lax.broadcasted_iota(jnp.int32, (half, own), 0).astype(F32) * (-2.0 * math.log(ROPE_BASE) / dim))
    angle = pos[:, cols].astype(F32) * freq
    cos_t, sin_t = jnp.cos(angle), jnp.sin(angle)
    bias = jnp.broadcast_to(bqkv[...].reshape(1, n_out).astype(F32), (128, n_out)).T
    lane[...] = jnp.broadcast_to(lens[...].astype(F32), lane.shape).astype(BF16)

    total = qown[...]
    for d in order:
        arrived(qrecv.at[d - 1], q_ids[d - 1])
        total = total + qrecv[d - 1].astype(F32)
    qkv = (total + bias[:, 0:1]).astype(BF16)

    def rotate(v):
        lo, up = v[:half].astype(F32), v[half:].astype(F32)
        return jnp.concatenate([lo * cos_t - up * sin_t, up * cos_t + lo * sin_t], axis=0).astype(BF16)

    for h in range(heads):
        base = 3 * h * dim
        qs[h] = rotate(qkv[base:base + dim]).astype(F32)
        kvn[0, h, :, cols] = rotate(qkv[base + dim:base + 2 * dim])
        kvn[1, h, :, cols] = qkv[base + 2 * dim:base + 3 * dim]

    def score_step(i, carry):
        for s in range(GROUP):
            for h in range(heads):
                sc[h, pl.ds(i * GROUP + s, 1), :] = jnp.sum(
                    kc[i * GROUP + s, h, :, cols].astype(F32) * qs[h], axis=0, keepdims=True)
        return carry

    for cp in cache_loads[0]:
        cp.wait()
    lax.fori_loop(0, total_slots // GROUP, score_step, 0)
    slot_id = lax.broadcasted_iota(jnp.int32, (total_slots, own), 0)
    own_len = lens[:, cols]
    ok, hit = slot_id <= own_len, slot_id == own_len
    p_new = []
    for h in range(heads):
        s_new = jnp.sum(kvn[0, h, :, cols].astype(F32) * qs[h], axis=0, keepdims=True)
        s = jnp.where(hit, s_new, sc[h]) * (dim ** -0.5)
        s = jnp.where(ok, s, -1e30)
        e = jnp.exp(s - jnp.max(s, axis=0, keepdims=True))
        p = (e / jnp.sum(e, axis=0, keepdims=True)).astype(BF16).astype(F32)
        p_new.append(jnp.sum(jnp.where(hit, p, 0.0), axis=0, keepdims=True))
        sc[h] = jnp.where(hit, 0.0, p)
    for h in range(heads):
        qs[h] = p_new[h] * kvn[1, h, :, cols].astype(F32)

    def mix_step(i, carry):
        for h in range(heads):
            a = qs[h]
            for s in range(GROUP):
                a = a + vc[i * GROUP + s, h, :, cols].astype(F32) * sc[h, pl.ds(i * GROUP + s, 1), :]
            qs[h] = a
        return carry

    for cp in cache_loads[1]:
        cp.wait()
    lax.fori_loop(0, total_slots // GROUP, mix_step, 0)
    attn = qs[...].reshape(heads * dim, own).T.astype(BF16)

    def update(ref, which):
        def write(i, carry):
            for s in range(GROUP):
                slot_hit = lane[...] == (i * GROUP + s).astype(F32).astype(BF16)
                for h in range(heads):
                    for t in range(dim // 16):
                        part = pl.ds(t * 16, 16)
                        ref[i * GROUP + s, h, part, :] = jnp.where(
                            slot_hit, kvn[which, h, part, :], ref[i * GROUP + s, h, part, :])
            return carry

        lax.fori_loop(0, total_slots // GROUP, write, 0)

    def vec(i):
        return vecs[i:i + 1, :]

    def scatter_sum(part, dbuf, sbuf, rbuf):
        base = ids(nc)
        start(part.at[1 - core], dbuf, base[0], partner)
        arrived(dbuf, base[0])
        sbuf[...] = (part[core].astype(F32) + dbuf[...].astype(F32)).astype(BF16)
        for d in (2, 1, 3):
            start(sbuf.at[chip_at(d)], rbuf.at[d - 1], base[d], chip_dev(d))
        sums = sbuf[chip].astype(F32)
        for d in range(1, nc):
            arrived(rbuf.at[d - 1], base[d])
            sums = sums + rbuf[d - 1].astype(F32)
        return sums

    def share(buf_at, meanwhile):
        far, near = ids(nc), ids(nc)
        for d in (2, 1, 3):
            start(buf_at(blk), buf_at(blk), far[d], chip_dev(d))
        start(buf_at(blk), buf_at(blk), near[0], partner)
        meanwhile()
        for d in (1, 3, 2):
            ref = buf_at(core * nc + chip_at(-d))
            arrived(ref, far[d])
            start(ref, ref, near[d], partner)
        for d in (0, 1, 3, 2):
            arrived(buf_at((1 - core) * nc + chip_at(-d)), near[d])

    def put(part, d, value):
        part[:, :, :, x_cols(d)] = value.astype(BF16).reshape(CORES, nc, per, width)

    put(part1, 0, jnp.dot(attn, wo_own[...], preferred_element_type=F32))
    for d in order:
        arrived(wo_far.at[d - 1], wo_ids[d - 1])
        put(part1, -d, jnp.dot(attn, wo_far[d - 1], preferred_element_type=F32))
    total = scatter_sum(part1, dbuf1, sbuf1, rbuf1)
    for d in range(1, nx):
        arrived(hid_own.at[:, x_cols(-d)], hid_ids[d - 1])
        arrived(vecs.at[:, x_cols(-d)], vec_ids[d - 1])
    h_attn = DEEP_ALPHA * hid_own[...].astype(F32) + total + vec(0)
    zall[blk] = layer_norm(h_attn, vec(1), vec(2))
    share(lambda b: zall.at[b], up_ring.forward)
    down_ring.forward()
    for d in order:
        mine = kvn.at[:, :, :, cols]
        start(mine, mine, kv_ids[d - 1], x_dev(d))

    ups = [(0, wup_own), (1, wup_far.at[0]), (-1, wup_far.at[2]), (2, wup_far.at[1])]
    downs = [(0, wdn_own), (1, wdn_far.at[0]), (-1, wdn_far.at[2]), (2, wdn_far.at[1])]
    gate = bup[0:1, :].astype(F32)
    val = bup[1:2, :].astype(F32)
    up_ring.near()
    for d, w in ups:
        if d == 2:
            up_ring.far()
        zb = zall[:, :, x_cols(d)].reshape(own, width)
        gate = gate + jnp.dot(zb, w[0], preferred_element_type=F32)
        val = val + jnp.dot(zb, w[1], preferred_element_type=F32)
    g = (jax.nn.gelu(gate, approximate=True) * val).astype(BF16)
    down_ring.near()
    for d, w in downs:
        if d == 2:
            down_ring.far()
        put(part2, d, jnp.dot(g, w[...], preferred_element_type=F32))
    total = scatter_sum(part2, dbuf2, sbuf2, rbuf2)
    h_mlp = DEEP_ALPHA * zall[blk].astype(F32) + total + vec(3)
    o = layer_norm(h_mlp, vec(4), vec(5))
    for b in range(nx):
        obuf[b] = o[:, b * width:(b + 1) * width]
    out_ids = ids(nx)
    for d in order:
        start(obuf.at[x_at(d)], out_ref.at[x, blk], out_ids[d], x_dev(d))
    out_ref[x, blk] = obuf[x]
    for d in range(1, nx):
        arrived(kvn.at[:, :, :, x_rows(-d)], kv_ids[d - 1])
    update(kc, 0)
    for d in range(1, nx):
        arrived(out_ref.at[x_at(-d), blk], out_ids[d])
    share(lambda b: out_ref.at[:, b], lambda: update(vc, 1))
    for cp in started:
        cp.wait_send()


def layer(nx, ny, hidden, w_qkv, w_out, w_up, w_down, b_up, b_qkv, positions, lengths, k_t, v_t, vecs):
    nc = ny // CORES
    rows, width = hidden.shape
    total_slots, heads, dim, _ = k_t.shape
    own = rows // nx
    per = own // ny
    total_width = width * nx
    n_out = w_qkv.shape[1]
    n_sem = 5 * (nx - 1) + 12 + 6 * nc + nx
    hbm = pl.BlockSpec(memory_space=pltpu.HBM)
    vm = pl.BlockSpec(memory_space=pltpu.VMEM)
    reduce_bufs = [pltpu.VMEM((CORES, nc, per, total_width), BF16), pltpu.VMEM((nc, per, total_width), BF16),
                   pltpu.VMEM((nc, per, total_width), BF16), pltpu.VMEM((nc - 1, per, total_width), BF16)]
    ins = (hidden, w_qkv, w_out, w_up, w_down, b_up, b_qkv, positions.reshape(1, rows), lengths.reshape(1, rows))
    out, k_t, v_t = pl.pallas_call(
        functools.partial(layer_kernel, nx, ny),
        out_shape=(jax.ShapeDtypeStruct((nx, ny, per, width), BF16), pltpu.VMEM(k_t.shape, BF16),
                   pltpu.VMEM(v_t.shape, BF16)),
        in_specs=[hbm] * (len(ins) + 2 + N_VEC),
        out_specs=(vm,) * 3,
        scratch_shapes=[pltpu.VMEM(v.shape, BF16) for v in vecs] + [
            pltpu.VMEM(a.shape, a.dtype) for a in (hidden, w_qkv, w_out, w_up, w_down, b_up, b_qkv, ins[7], ins[8])] + [
            pltpu.VMEM((nx - 1, n_out, own), BF16), pltpu.VMEM((nx - 1, n_out, own), BF16),
            pltpu.VMEM((n_out, own), F32), pltpu.VMEM((2, heads, dim, rows), BF16),
            pltpu.VMEM((heads, dim, own), F32), pltpu.VMEM((heads, total_slots, own), F32),
            pltpu.VMEM((16, rows), BF16), pltpu.VMEM((nx - 1,) + w_out.shape, BF16),
            pltpu.VMEM((nx - 1,) + w_up.shape, BF16), pltpu.VMEM((nx - 1,) + w_down.shape, BF16),
            pltpu.VMEM((8, width), F32), pltpu.VMEM((8, total_width), F32), pltpu.VMEM((per, total_width), BF16),
        ] + reduce_bufs + reduce_bufs + [
            pltpu.VMEM((ny, per, total_width), BF16), pltpu.VMEM((nx, per, width), BF16),
            pltpu.SemaphoreType.DMA((n_sem,)), pltpu.SemaphoreType.DMA((n_sem,)),
            pltpu.SemaphoreType.DMA((len(ins) + N_VEC,)), pltpu.SemaphoreType.DMA((2, N_LOAD))],
        compiler_params=pltpu.CompilerParams(collective_id=0, has_side_effects=True, vmem_limit_bytes=24 * 2**20),
        name='layer',
    )(*ins, k_t, v_t, *vecs)
    return out.reshape(rows, width), k_t, v_t


def solution(mesh):
    nx, ny = mesh.shape['x'], mesh.shape['y']
    cache_spec = P('dp', None, 'y', None)
    width_spec = P('x')
    in_specs = (P('dp', 'x'), P('x', 'y'), P('y'), P('y', 'x'), width_spec, width_spec, width_spec, P('x', None, 'y'), P(None, 'y'), P('y', 'x'), width_spec, width_spec, width_spec, cache_spec, cache_spec, P('dp'), P('dp'))
    out_specs = (P('dp', 'x'), cache_spec, cache_spec)

    def local_step(hidden, w_qkv, b_qkv, w_out, b_out, attn_gain, attn_shift, w_up, b_up, w_down, b_down, mlp_gain, mlp_shift, k_cache, v_cache, positions, lengths):
        k_t, v_t = jnp.transpose(k_cache, (1, 2, 3, 0)), jnp.transpose(v_cache, (1, 2, 3, 0))
        w_up = jnp.transpose(w_up, (1, 0, 2))
        vecs = (b_out, attn_gain, attn_shift, b_down, mlp_gain, mlp_shift)
        result, k_t, v_t = layer(nx, ny, hidden, w_qkv, w_out, w_up, w_down, b_up, b_qkv, positions, lengths, k_t, v_t, vecs)
        k_full, v_full = jnp.transpose(k_t, (3, 0, 1, 2)), jnp.transpose(v_t, (3, 0, 1, 2))
        return result, k_full, v_full

    return jax.shard_map(local_step, mesh=mesh, in_specs=in_specs, out_specs=out_specs, check_vma=False)
```

time: 295 us -> 81.6 us (0.28); the launches traced: 292 us -> 81.4 us
  waiting for transfers between devices: 204 us -> 0 us
  Pallas kernels: 0 us -> 65.7 us
  other arithmetic: 48 us -> 0 us
  blocking collectives: 17.3 us -> 0 us
  local copies, waits for them, and re-layouts: 0.76 us -> 15 us
  between operations: 14.1 us -> 0.64 us
  matrix products: 7.27 us -> 0 us
    psum x4 -> x0, waiting for transfers between devices: 204 us -> none  [the longest x1 56.3 us: local_step(): proj_sum = lax.psum(proj_part, 'y')]
    pallas_call x0 -> x1, Pallas kernels: none -> 65.7 us  [layer(): pl.pallas_call(functools.partial(layer_kernel, nx, ny), out_shape=(jax.Sh...]
    dot_general x1 -> x0, other arithmetic: 17.7 us -> none  [attend(): jnp.einsum('bhs,bshd->bhd', attn_probs, v_full, preferred_element_type=jn...]
    psum x2 -> x0, blocking collectives: 17.3 us -> none  [sharded_norm(): moments = lax.psum(moments, 'x')]
    unnamed x2 -> x0, other arithmetic: 17 us -> none
    unnamed x23 -> x6, local copies, waits for them, and re-layouts: 0.47 us -> 15 us
    dot_general x4 -> x0, matrix products: 7.27 us -> none  [the longest x1 2.44 us: local_step(): jnp.dot(hidden, w_qkv, preferred_element_type=jnp.float32)]
    convert_element_type x12 -> x0, other arithmetic: 6.26 us -> none  [the longest x2 3.58 us: sharded_norm(): (scaled * gain.astype(jnp.float32) + shift.astype(jnp.float32)).astype(jn...]
  transfers between devices with their start and end apart: 4 -> 0, of which waited for: 4 -> 0; matrix products, arithmetic and copies ran while one was open for 1% -> 0% of each run, Pallas kernels for 0% -> 0%
where the time goes in v5:
time: 81.6 us; the launch traced here: 81.4 us
  Pallas kernels  65.7 us (81%)
  local copies, waits for them, and re-layouts  15 us (18%)
    pallas_call x1, Pallas kernels, layer(): pl.pallas_call(functools.partial(layer_kernel, nx, ny), out_shape=(jax.Sh...  65.7 us
    unnamed x6, local copies, waits for them, and re-layouts  15 us

profile of v5, /device:TPU:97, one launch (start us, length us, event | category | flops | bytes accessed | tf_op | source)
XLA Modules:
  0.0 81.4 jit_solution(5401873738805834080)
XLA Ops:
  0.6 1.9 %copy.22 = bf16[256,2,512]{2,0,1:T(8,128)(2,1)} copy(bf16[256,2,512]{2,1,0:T(2,128)(2,1)} %param.24) | data formatting | bytes 1048576 | tf_op args[7]
  2.5 65.7 %layer.1 = (bf16[4,8,32,256]{3,2,1,0:T(8,128)(2,1)}, bf16[64,2,64,1024]{3,2,1,0:T(8,128)(2,1)S(1)}, bf16[64,2,64,1024]{3,2,1,0:T(8,128)(2,1)S(1)}) custom-call(bf16[1024,256]{1,0:T(8,128)(2,1)} %hid_in.1, bf16[256,384]{1,0:T(8,128)(2,1)} %wqkv_in.1, bf16[128,256]{1,0:T(8,128)(2,1)} %wo_in.1, bf16[2,256,512]{2,1,0:T(8,128)(2,1)} %bitcast.14, ...), custom_call_target="tpu_custom_call" | custom-call | tf_op jit(solution)/shard_map/layer/pallas_call | solution.py:334
  68.3 6.2 %copy.26 = bf16[1024,64,2,64]{0,3,2,1:T(8,128)(2,1)} copy(bf16[1024,64,2,64]{0,3,2,1:T(8,128)(2,1)S(1)} %bitcast.11) | data formatting | bytes 33554432
  74.4 0.0 copy-start
  74.4 6.2 %copy.27 = bf16[1024,64,2,64]{0,3,2,1:T(8,128)(2,1)} copy(bf16[1024,64,2,64]{0,3,2,1:T(8,128)(2,1)S(1)} %bitcast.10) | data formatting | bytes 33554432
  80.6 0.0 copy-done
  80.6 0.8 copy.28
Async XLA Ops:
  74.4 6.2 %copy-start = (bf16[4,8,32,256]{3,2,1,0:T(8,128)(2,1)S(1)}, bf16[4,8,32,256]{3,2,1,0:T(8,128)(2,1)}, u32[]{:S(2)}) copy-start(bf16[4,8,32,256]{3,2,1,0:T(8,128)(2,1)} %get-tuple-element.6) | copy-start | bytes 1572868

commit v6 on v5

--- a/solution.py
+++ b/solution.py
@@ -30,8 +30,8 @@
     vec_in, refs = refs[:N_VEC], refs[N_VEC:]
     out_ref, kc, vc = refs[:3]
     vec_own, refs = refs[3:3 + N_VEC], refs[3 + N_VEC:]
-    (hid, wqkv, wo_own, wup_own, wdn_own, bup, bqkv, pos, lens, qpart, qrecv, qown, kvn, qs, sc, lane,
-     wo_far, wup_far, wdn_far, vloc, vecs, hid_own, part1, dbuf1, sbuf1, rbuf1, part2, dbuf2, sbuf2, rbuf2,
+    (hid, wqkv, wo_own, wup_raw, wdn_own, bup, bqkv, pos, lens, qpart, qrecv, qown, kvn, qs, sc, lane,
+     wo_far, wup_own, wup_far, wdn_far, vloc, vecs, hid_own, part1, dbuf1, sbuf1, rbuf1, part2, dbuf2, sbuf2, rbuf2,
      zall, obuf, send, recv, load, cache_load) = refs
     nc = ny // CORES
     x, y = lax.axis_index('x'), lax.axis_index('y')
@@ -57,6 +57,9 @@
     def x_dev(d):
         return {'x': x_at(d)}
 
+    def grid_dev(dx, dc):
+        return {'x': x_at(dx), 'y': chip_at(dc) * CORES + core}
+
     def x_cols(d):
         return pl.ds(pl.multiple_of(x_at(d) * width, width), width)
 
@@ -84,7 +87,7 @@
         copy(ref, ref, i, partner).wait_recv()
 
     pairs = [(hid_in, hid), (wqkv_in, wqkv), (bqkv_in, bqkv), (pos_in, pos), (lens_in, lens), (bup_in, bup),
-             (wo_in, wo_own), (wup_in, wup_own), (wdn_in, wdn_own)] + list(zip(vec_in, vec_own))
+             (wo_in, wo_own), (wup_in, wup_raw), (wdn_in, wdn_own)] + list(zip(vec_in, vec_own))
     loads = [pltpu.make_async_copy(src, dst, load.at[i]) for i, (src, dst) in enumerate(pairs)]
     for cp in loads:
         cp.start()
@@ -94,7 +97,8 @@
                    for j, (src, dst) in enumerate(((k_in, kc), (v_in, vc)))]
 
     barrier = pltpu.get_barrier_semaphore()
-    peers = [partner] + [chip_dev(d) for d in range(1, nc)] + [x_dev(d) for d in range(1, nx)]
+    grid = [(dx, dc) for dx in (2, 1, 3, 0) for dc in (2, 1, 3, 0) if dx or dc]
+    peers = [partner] + [grid_dev(dx, dc) for dx, dc in grid]
     for dev in peers:
         pl.semaphore_signal(barrier, inc=1, device_id=dev, device_id_type=MESH)
     for cp in loads:
@@ -131,6 +135,8 @@
         def begin(self):
             start(self.piece(0), self.buf(2, 0), self.ra, x_dev(1))
             start(self.piece(1), self.buf(0, 1), self.lb, x_dev(-1))
+
+        def rest(self):
             start(self.piece(1), self.buf(2, 1), self.rb, x_dev(1))
             start(self.piece(0), self.buf(0, 0), self.la, x_dev(-1))
 
@@ -151,8 +157,9 @@
     hd = wdn_own.shape[0] // 2
     up_ring = Ring(lambda h: wup_own.at[h], lambda s, h: wup_far.at[s, h])
     down_ring = Ring(lambda h: wdn_own.at[pl.ds(h * hd, hd)], lambda s, h: wdn_far.at[s, pl.ds(h * hd, hd)])
+    for i in range(2):
+        wup_own[i] = wup_raw[:, i, :]
     up_ring.begin()
-    down_ring.begin()
     for group in cache_loads:
         for cp in group:
             cp.start()
@@ -236,13 +243,14 @@
     def vec(i):
         return vecs[i:i + 1, :]
 
-    def scatter_sum(part, dbuf, sbuf, rbuf):
+    def scatter_sum(part, dbuf, sbuf, rbuf, meanwhile):
         base = ids(nc)
         start(part.at[1 - core], dbuf, base[0], partner)
         arrived(dbuf, base[0])
         sbuf[...] = (part[core].astype(F32) + dbuf[...].astype(F32)).astype(BF16)
         for d in (2, 1, 3):
             start(sbuf.at[chip_at(d)], rbuf.at[d - 1], base[d], chip_dev(d))
+        meanwhile()
         sums = sbuf[chip].astype(F32)
         for d in range(1, nc):
             arrived(rbuf.at[d - 1], base[d])
@@ -269,17 +277,17 @@
     for d in order:
         arrived(wo_far.at[d - 1], wo_ids[d - 1])
         put(part1, -d, jnp.dot(attn, wo_far[d - 1], preferred_element_type=F32))
-    total = scatter_sum(part1, dbuf1, sbuf1, rbuf1)
+    total = scatter_sum(part1, dbuf1, sbuf1, rbuf1, lambda: (up_ring.rest(), down_ring.begin()))
     for d in range(1, nx):
         arrived(hid_own.at[:, x_cols(-d)], hid_ids[d - 1])
         arrived(vecs.at[:, x_cols(-d)], vec_ids[d - 1])
     h_attn = DEEP_ALPHA * hid_own[...].astype(F32) + total + vec(0)
     zall[blk] = layer_norm(h_attn, vec(1), vec(2))
-    share(lambda b: zall.at[b], up_ring.forward)
-    down_ring.forward()
-    for d in order:
-        mine = kvn.at[:, :, :, cols]
-        start(mine, mine, kv_ids[d - 1], x_dev(d))
+    def send_weights():
+        up_ring.forward()
+        down_ring.rest()
+
+    share(lambda b: zall.at[b], send_weights)
 
     ups = [(0, wup_own), (1, wup_far.at[0]), (-1, wup_far.at[2]), (2, wup_far.at[1])]
     downs = [(0, wdn_own), (1, wdn_far.at[0]), (-1, wdn_far.at[2]), (2, wdn_far.at[1])]
@@ -289,6 +297,7 @@
     for d, w in ups:
         if d == 2:
             up_ring.far()
+            down_ring.forward()
         zb = zall[:, :, x_cols(d)].reshape(own, width)
         gate = gate + jnp.dot(zb, w[0], preferred_element_type=F32)
         val = val + jnp.dot(zb, w[1], preferred_element_type=F32)
@@ -298,21 +307,29 @@
         if d == 2:
             down_ring.far()
         put(part2, d, jnp.dot(g, w[...], preferred_element_type=F32))
-    total = scatter_sum(part2, dbuf2, sbuf2, rbuf2)
+    def send_kv():
+        for d in order:
+            own_kv = kvn.at[:, :, :, cols]
+            start(own_kv, own_kv, kv_ids[d - 1], x_dev(d))
+
+    total = scatter_sum(part2, dbuf2, sbuf2, rbuf2, send_kv)
     h_mlp = DEEP_ALPHA * zall[blk].astype(F32) + total + vec(3)
     o = layer_norm(h_mlp, vec(4), vec(5))
     for b in range(nx):
         obuf[b] = o[:, b * width:(b + 1) * width]
-    out_ids = ids(nx)
-    for d in order:
-        start(obuf.at[x_at(d)], out_ref.at[x, blk], out_ids[d], x_dev(d))
+    out_ids = ids(nx * nc + 1)
+    for dx, dc in grid:
+        start(obuf.at[x_at(dx)], out_ref.at[x, blk], out_ids[dx * nc + dc], grid_dev(dx, dc))
     out_ref[x, blk] = obuf[x]
     for d in range(1, nx):
         arrived(kvn.at[:, :, :, x_rows(-d)], kv_ids[d - 1])
     update(kc, 0)
-    for d in range(1, nx):
-        arrived(out_ref.at[x_at(-d), blk], out_ids[d])
-    share(lambda b: out_ref.at[:, b], lambda: update(vc, 1))
+    update(vc, 1)
+    for dx, dc in grid:
+        arrived(out_ref.at[x_at(-dx), core * nc + chip_at(-dc)], out_ids[dx * nc + dc])
+    mine = out_ref.at[:, pl.ds(core * nc, nc)]
+    start(mine, mine, out_ids[nx * nc], partner)
+    arrived(out_ref.at[:, pl.ds((1 - core) * nc, nc)], out_ids[nx * nc])
     for cp in started:
         cp.wait_send()
 
@@ -325,7 +342,8 @@
     per = own // ny
     total_width = width * nx
     n_out = w_qkv.shape[1]
-    n_sem = 5 * (nx - 1) + 12 + 6 * nc + nx
+    up_shape = (w_up.shape[1], w_up.shape[0], w_up.shape[2])
+    n_sem = 5 * (nx - 1) + 12 + 4 * nc + nx * nc + 1
     hbm = pl.BlockSpec(memory_space=pltpu.HBM)
     vm = pl.BlockSpec(memory_space=pltpu.VMEM)
     reduce_bufs = [pltpu.VMEM((CORES, nc, per, total_width), BF16), pltpu.VMEM((nc, per, total_width), BF16),
@@ -343,7 +361,7 @@
             pltpu.VMEM((n_out, own), F32), pltpu.VMEM((2, heads, dim, rows), BF16),
             pltpu.VMEM((heads, dim, own), F32), pltpu.VMEM((heads, total_slots, own), F32),
             pltpu.VMEM((16, rows), BF16), pltpu.VMEM((nx - 1,) + w_out.shape, BF16),
-            pltpu.VMEM((nx - 1,) + w_up.shape, BF16), pltpu.VMEM((nx - 1,) + w_down.shape, BF16),
+            pltpu.VMEM(up_shape, BF16), pltpu.VMEM((nx - 1,) + up_shape, BF16), pltpu.VMEM((nx - 1,) + w_down.shape, BF16),
             pltpu.VMEM((8, width), F32), pltpu.VMEM((8, total_width), F32), pltpu.VMEM((per, total_width), BF16),
         ] + reduce_bufs + reduce_bufs + [
             pltpu.VMEM((ny, per, total_width), BF16), pltpu.VMEM((nx, per, width), BF16),
@@ -364,7 +382,6 @@
 
     def local_step(hidden, w_qkv, b_qkv, w_out, b_out, attn_gain, attn_shift, w_up, b_up, w_down, b_down, mlp_gain, mlp_shift, k_cache, v_cache, positions, lengths):
         k_t, v_t = jnp.transpose(k_cache, (1, 2, 3, 0)), jnp.transpose(v_cache, (1, 2, 3, 0))
-        w_up = jnp.transpose(w_up, (1, 0, 2))
         vecs = (b_out, attn_gain, attn_shift, b_down, mlp_gain, mlp_shift)
         result, k_t, v_t = layer(nx, ny, hidden, w_qkv, w_out, w_up, w_down, b_up, b_qkv, positions, lengths, k_t, v_t, vecs)
         k_full, v_full = jnp.transpose(k_t, (3, 0, 1, 2)), jnp.transpose(v_t, (3, 0, 1, 2))

time: 81.6 us -> 78.5 us (0.962)
  local copies, waits for them, and re-layouts: 15 us -> 13.1 us
  Pallas kernels: 65.7 us -> 64.6 us
    unnamed x6 -> x5, local copies, waits for them, and re-layouts: 15 us -> 13.1 us
    pallas_call x1, Pallas kernels: 65.7 us -> 64.6 us  [layer(): pl.pallas_call(functools.partial(layer_kernel, nx, ny), out_shape=(jax.Sh...]
where the time goes in v6:
time: 78.5 us; the launch traced here: 78.3 us
  Pallas kernels  64.6 us (82%)
  local copies, waits for them, and re-layouts  13.1 us (17%)
    pallas_call x1, Pallas kernels, layer(): pl.pallas_call(functools.partial(layer_kernel, nx, ny), out_shape=(jax.Sh...  64.6 us
    unnamed x5, local copies, waits for them, and re-layouts  13.1 us

profile of v6, /device:TPU:97, one launch (start us, length us, event | category | flops | bytes accessed | tf_op | source)
XLA Modules:
  0.0 78.3 jit_solution(2233844627781696540)
XLA Ops:
  0.6 64.6 %layer.1 = (bf16[4,8,32,256]{3,2,1,0:T(8,128)(2,1)}, bf16[64,2,64,1024]{3,2,1,0:T(8,128)(2,1)S(1)}, bf16[64,2,64,1024]{3,2,1,0:T(8,128)(2,1)S(1)}) custom-call(bf16[1024,256]{1,0:T(8,128)(2,1)} %hid_in.1, bf16[256,384]{1,0:T(8,128)(2,1)} %wqkv_in.1, bf16[128,256]{1,0:T(8,128)(2,1)} %wo_in.1, bf16[256,2,512]{2,1,0:T(2,128)(2,1)} %wup_in.1, ...), custom_call_target="tpu_custom_call" | custom-call | tf_op jit(solution)/shard_map/layer/pallas_call | solution.py:352
  65.2 6.2 %copy.23 = bf16[1024,64,2,64]{0,3,2,1:T(8,128)(2,1)} copy(bf16[1024,64,2,64]{0,3,2,1:T(8,128)(2,1)S(1)} %bitcast.8) | data formatting | bytes 33554432
  71.4 0.0 copy-start
  71.4 6.2 %copy.24 = bf16[1024,64,2,64]{0,3,2,1:T(8,128)(2,1)} copy(bf16[1024,64,2,64]{0,3,2,1:T(8,128)(2,1)S(1)} %bitcast.7) | data formatting | bytes 33554432
  77.6 0.0 copy-done
  77.6 0.8 %copy.25 = bf16[1024,256]{1,0:T(8,128)(2,1)} copy(bf16[1024,256]{1,0:T(8,128)(2,1)S(1)} %bitcast.11) | data formatting | bytes 1048576
Async XLA Ops:
  71.4 6.2 %copy-start = (bf16[4,8,32,256]{3,2,1,0:T(8,128)(2,1)S(1)}, bf16[4,8,32,256]{3,2,1,0:T(8,128)(2,1)}, u32[]{:S(2)}) copy-start(bf16[4,8,32,256]{3,2,1,0:T(8,128)(2,1)} %get-tuple-element.6) | copy-start | bytes 1572868
